TPU v7x, 32 devices: a whole 2x2x4 slice. The times are simulated.
32 devices in a mesh: rep: 4 (over x, y), dp: 8 (over z, core).
Axes of the slice: x: 2, y: 2, z: 4, core: 2. Of those that a mesh axis runs over, the one named last changes fastest.
Arguments:
- x: bfloat16 [32, 2048, 640], P(('rep', 'dp')), parts along dimension 0
- dy: bfloat16 [32, 2048, 640], P(('rep', 'dp')), parts along dimension 0
- w_gate: bfloat16 [2, 640, 4096], replicated
- w_up: bfloat16 [2, 640, 4096], replicated
- w_down: bfloat16 [2, 4096, 640], replicated
- m_w_gate: float32 [2, 640, 4096], P(None, 'dp')
- m_w_up: float32 [2, 640, 4096], P(None, 'dp')
- m_w_down: float32 [2, 4096, 640], P(None, 'dp')
- v_w_gate: float32 [2, 640, 4096], P(None, 'dp')
- v_w_up: float32 [2, 640, 4096], P(None, 'dp')
- v_w_down: float32 [2, 4096, 640], P(None, 'dp')
Outputs:
- output 1: bfloat16 [8, 640, 4096], P('rep'), parts along dimension 0
- output 2: bfloat16 [8, 640, 4096], P('rep'), parts along dimension 0
- output 3: bfloat16 [8, 4096, 640], P('rep'), parts along dimension 0
- output 4: float32 [8, 640, 4096], P('rep', 'dp'), parts along dimension 0
- output 5: float32 [8, 640, 4096], P('rep', 'dp'), parts along dimension 0
- output 6: float32 [8, 4096, 640], P('rep', 'dp'), parts along dimension 0
- output 7: float32 [8, 640, 4096], P('rep', 'dp'), parts along dimension 0
- output 8: float32 [8, 640, 4096], P('rep', 'dp'), parts along dimension 0
- output 9: float32 [8, 4096, 640], P('rep', 'dp'), parts along dimension 0
There are 4 independent parts. A program takes and returns all parts, laid end to end along the dimension named above; an argument that names none is the same for every part.
All inputs are finite; a program needn't handle non-finite values.
Results may differ from a plain program's by a relative error of at most 0.022.
Values are sent between devices in bfloat16 or wider.
A program may use at most 2 GiB of HBM per device.

v0:
```python
import jax
import jax.numpy as jnp
from jax import lax

NAMES = ("w_gate", "w_up", "w_down")


def matmul(a, w):
    return jnp.dot(a, w, preferred_element_type=jnp.float32).astype(jnp.bfloat16)


def normed(h):
    wide = h.astype(jnp.float32)
    scale = lax.rsqrt(jnp.mean(wide**2, -1, keepdims=True) + 1e-6)
    return (wide * scale).astype(jnp.bfloat16)


def layer(h, w):
    a = normed(h)
    gate = jnp.dot(a, w["w_gate"], preferred_element_type=jnp.float32)
    up = jnp.dot(a, w["w_up"], preferred_element_type=jnp.float32)
    return h + matmul((jax.nn.silu(gate) * up).astype(jnp.bfloat16), w["w_down"])


def adamw(w, m, v, g):
    m = 0.9 * m + 0.1 * g
    v = 0.95 * v + 0.05 * g * g
    step = m * lax.rsqrt(v + 1e-8) + 0.1 * w
    return (w - 0.02 * step).astype(jnp.bfloat16), m, v


def stack(weights, h):
    for number in range(weights["w_gate"].shape[0]):
        h = layer(h, {name: w[number] for name, w in weights.items()})
    return h


def solution(mesh):
    groups = mesh.shape["rep"]

    def step(x, dy, *arrays):
        weights, m, v = (arrays[i : i + 3] for i in (0, 3, 6))
        x, dy = (t.reshape(groups, -1, *t.shape[1:]) for t in (x, dy))

        def of_a_group(x, dy):
            _, back = jax.vjp(lambda w: stack(w, x), dict(zip(NAMES, weights, strict=True)))
            by_weights = back(dy)[0]
            gradients = [by_weights[name].astype(jnp.float32) for name in NAMES]
            new = [adamw(w.astype(jnp.float32), m, v, g) for w, m, v, g in zip(weights, m, v, gradients, strict=True)]
            return tuple(one[which] for which in range(3) for one in new)

        return tuple(t.reshape(-1, *t.shape[2:]) for t in jax.vmap(of_a_group)(x, dy))

    return step
```

profile of v0, /device:TPU:0, one launch (start us, length us, event | category | flops | bytes accessed | tf_op | source)
XLA Modules:
  0.0 1259.6 jit_solution(13885648692359630868)
XLA Ops:
  9.7 4.4 copy
  14.1 19.9 %fusion.67 = f32[2048,4096]{1,0:T(8,128)} fusion(bf16[2,640,4096]{2,1,0:T(8,128)(2,1)} %param, bf16[1,2048,640]{2,1,0:T(8,128)(2,1)S(1)} %copy-done, f32[2048]{0:T(1024)S(1)} %add_rsqrt_fusion), kind=kOutput, calls=%fused_computation.78 | convolution fusion | flops 10741350400 | bytes 41426944 | tf_op jit(solution)/vmap(jvp())/dot_general | solution.py:20
  34.0 19.9 %fusion.65 = f32[2048,4096]{1,0:T(8,128)} fusion(bf16[2,640,4096]{2,1,0:T(8,128)(2,1)} %param.3, bf16[1,2048,640]{2,1,0:T(8,128)(2,1)S(1)} %copy-done, f32[2048]{0:T(1024)S(1)} %add_rsqrt_fusion), kind=kOutput, calls=%fused_computation.76 | convolution fusion | flops 10741350400 | bytes 41426944 | tf_op jit(solution)/vmap(jvp())/dot_general | solution.py:21
  53.9 27.5 %fusion.26 = bf16[2048,4096]{1,0:T(8,128)(2,1)} fusion(f32[2048,4096]{1,0:T(8,128)} %fusion.65, f32[2048,4096]{1,0:T(8,128)} %fusion.67), kind=kLoop, calls=%fused_computation.35 | loop fusion | flops 50331648 | bytes 83886080
  81.5 16.8 %fusion.51 = (f32[2048]{0:T(1024)S(1)}, bf16[1,1,2048,640]{2,3,1,0:T(8,128)(2,1)S(1)}) fusion(bf16[2048,4096]{1,0:T(8,128)(2,1)} %fusion.26, bf16[2,4096,640]{2,1,0:T(8,128)(2,1)} %param.4, bf16[1,2048,640]{1,2,0:T(8,128)(2,1)} %copy), kind=kOutput, calls=%fused_computation.62 | convolution fusion | flops 10743969792 | bytes 27271168 | tf_op jit(solution)/vmap(jvp())/dot_general | solution.py:9
  99.0 20.0 %fusion.54 = f32[2048,4096]{1,0:T(8,128)} fusion(bf16[2,640,4096]{2,1,0:T(8,128)(2,1)} %param, bf16[1,1,2048,640]{2,3,1,0:T(8,128)(2,1)S(1)} %get-tuple-element.10, f32[2048]{0:T(1024)S(1)} %bitcast.370), kind=kOutput, calls=%fused_computation.65 | convolution fusion | flops 10741350400 | bytes 41426944 | tf_op jit(solution)/vmap(jvp())/dot_general | solution.py:20
  119.0 19.7 %fusion.58 = f32[2048,4096]{1,0:T(8,128)} fusion(bf16[2,640,4096]{2,1,0:T(8,128)(2,1)} %param.3, bf16[1,1,2048,640]{2,3,1,0:T(8,128)(2,1)S(1)} %get-tuple-element.10, f32[2048]{0:T(1024)S(1)} %bitcast.371), kind=kOutput, calls=%fused_computation.69 | convolution fusion | flops 10741350400 | bytes 41426944 | tf_op jit(solution)/vmap(jvp())/dot_general | solution.py:21
  138.7 19.6 %convolution_convert_fusion.1 = bf16[2048,4096]{1,0:T(8,128)(2,1)} fusion(bf16[2,4096,640]{2,1,0:T(8,128)(2,1)} %param.4, bf16[1,2048,640]{2,1,0:T(8,128)(2,1)} %param.5), kind=kOutput, calls=%fused_computation.44 | convolution fusion | flops 10745806848 | bytes 24641536 | tf_op jit(solution)/vmap(transpose(jvp()))/dot_general | solution.py:9
  161.3 33.1 %fusion.6 = bf16[2048,4096]{1,0:T(8,128)(2,1)} fusion(f32[2048,4096]{1,0:T(8,128)} %fusion.54, f32[2048,4096]{1,0:T(8,128)} %fusion.58, bf16[2048,4096]{1,0:T(8,128)(2,1)} %convolution_convert_fusion.1), kind=kLoop, calls=%fused_computation.11 | loop fusion | flops 100663296 | bytes 100663296
  194.4 17.3 %fusion.78 = bf16[2048,640]{0,1:T(8,128)(2,1)} fusion(bf16[2048,4096]{1,0:T(8,128)(2,1)} %fusion.6, bf16[2,640,4096]{2,1,0:T(8,128)(2,1)} %param), kind=kOutput, calls=%fused_computation.102 | convolution fusion | flops 10737418240 | bytes 24641536 | tf_op jit(solution)/vmap(transpose(jvp()))/dot_general | solution.py:20
  211.7 24.8 %fusion.53 = (f32[2048]{0:T(1024)S(1)}, bf16[1,1,2048,640]{2,3,1,0:T(8,128)(2,1)}) fusion(bf16[1,1,2048,640]{2,3,1,0:T(8,128)(2,1)S(1)} %copy-done.2, bf16[2048,640]{0,1:T(8,128)(2,1)} %fusion.78, bf16[2,640,4096]{2,1,0:T(8,128)(2,1)} %param.3, bf16[2048,4096]{1,0:T(8,128)(2,1)} %convolution_convert_fusion.1, f32[2048,4096]{1,0:T(8,128)} %fusion.54), kind=kOutput, calls=%fused_computation.64 | convolution fusion | flops 10795612160 | bytes 63447040 | tf_op jit(solution)/vmap(transpose(jvp()))/dot_general | solution.py:21
  241.6 19.0 %convolution_bitcast_fusion = f32[1,4096,640]{2,1,0:T(8,128)} fusion(bf16[2048,4096]{1,0:T(8,128)(2,1)} %fusion.26, bf16[2048,640]{0,1:T(8,128)(2,1)S(1)} %fusion.129), kind=kOutput, calls=%fused_computation.49 | convolution fusion | flops 10737418240 | bytes 29884416 | tf_op jit(solution)/vmap(transpose(jvp()))/dot_general | solution.py:9
  262.4 28.7 %fusion.35 = f32[1,4096,640]{2,1,0:T(8,128)} fusion(f32[2048,4096]{1,0:T(8,128)} %fusion.58, f32[2048,4096]{1,0:T(8,128)} %fusion.54, bf16[1,2048,640]{2,1,0:T(8,128)(2,1)S(1)} %copy-done.6), kind=kOutput, calls=%fused_computation.50 | convolution fusion | flops 10787749888 | bytes 80216064 | tf_op jit(solution)/vmap(transpose(jvp()))/dot_general | solution.py:9
  292.8 18.6 %convolution_convert_fusion = bf16[2048,4096]{1,0:T(8,128)(2,1)} fusion(bf16[2048,640]{0,1:T(8,128)(2,1)S(1)} %copy-done.5, bf16[2,4096,640]{2,1,0:T(8,128)(2,1)} %param.4), kind=kOutput, calls=%fused_computation.43 | convolution fusion | flops 10745806848 | bytes 24641536 | tf_op jit(solution)/vmap(transpose(jvp()))/dot_general | solution.py:9
  311.4 25.6 %fusion.44 = f32[1,640,4096]{2,1,0:T(8,128)} fusion(bf16[2048,4096]{1,0:T(8,128)(2,1)} %convolution_convert_fusion, f32[2048,4096]{1,0:T(8,128)} %fusion.67, bf16[1,2048,640]{1,2,0:T(8,128)(2,1)} %copy, f32[2048]{0:T(1024)S(1)} %copy-done.17), kind=kOutput, calls=%fused_computation.53 | convolution fusion | flops 10791682048 | bytes 63447040 | tf_op jit(solution)/vmap(transpose(jvp()))/dot_general | solution.py:21
  338.8 25.1 %fusion.38 = f32[1,640,4096]{2,1,0:T(8,128)} fusion(bf16[2048,4096]{1,0:T(8,128)(2,1)} %convolution_convert_fusion.1, f32[2048,4096]{1,0:T(8,128)} %fusion.54, bf16[1,1,2048,640]{2,3,1,0:T(8,128)(2,1)S(1)} %copy-done.3, f32[2048]{0:T(1024)S(1)} %bitcast.373), kind=kOutput, calls=%fused_computation.51 | convolution fusion | flops 10791682048 | bytes 63447040 | tf_op jit(solution)/vmap(transpose(jvp()))/dot_general | solution.py:21
  364.0 16.9 %convolution_bitcast_fusion.1 = f32[1,640,4096]{2,1,0:T(8,128)} fusion(bf16[2048,4096]{1,0:T(8,128)(2,1)} %fusion.6, bf16[1,1,2048,640]{2,3,1,0:T(8,128)(2,1)S(1)} %copy-done.3, f32[2048]{0:T(1024)S(1)} %bitcast.374), kind=kOutput, calls=%fused_computation.54 | convolution fusion | flops 10741350400 | bytes 29892608 | tf_op jit(solution)/vmap(transpose(jvp()))/dot_general | solution.py:20
  382.6 34.4 %fusion.41 = f32[1,640,4096]{2,1,0:T(8,128)} fusion(f32[2048,4096]{1,0:T(8,128)} %fusion.67, f32[2048,4096]{1,0:T(8,128)} %fusion.65, bf16[2048,4096]{1,0:T(8,128)(2,1)} %convolution_convert_fusion, bf16[1,2048,640]{1,2,0:T(8,128)(2,1)S(1)} %copy-done.7, f32[2048]{0:T(1024)S(1)} %copy-done.17), kind=kOutput, calls=%fused_computation.52 | convolution fusion | flops 10833625088 | bytes 97001472 | tf_op jit(solution)/vmap(transpose(jvp()))/dot_general | solution.py:20
  420.3 62.6 %reduce-scatter.27.cloned.1.call-done = f32[1,512,640]{2,1,0:T(8,128)} async-done(((f32[1,4096,640]{2,1,0:T(8,128)}), f32[1,512,640]{2,1,0:T(8,128)}) %reduce-scatter.27.cloned.1.call-update) | async-done | bytes 1310736
  484.3 6.3 fusion.142
  490.7 103.0 %reduce-scatter.25.cloned.1.call-done = f32[1,80,4096]{2,1,0:T(8,128)} async-done(((f32[1,640,4096]{2,1,0:T(8,128)}), f32[1,80,4096]{2,1,0:T(8,128)}) %reduce-scatter.25.cloned.1.call-update) | async-done | bytes 1310736
  595.1 108.7 %reduce-scatter.23.cloned.1.call-done = f32[1,80,4096]{2,1,0:T(8,128)} async-done(((f32[1,640,4096]{2,1,0:T(8,128)}), f32[1,80,4096]{2,1,0:T(8,128)}) %reduce-scatter.23.cloned.1.call-update) | async-done | bytes 1310736
  705.2 6.3 fusion.143
  711.9 102.6 %reduce-scatter.19.cloned.1.call-done = f32[1,80,4096]{2,1,0:T(8,128)} async-done(((f32[1,640,4096]{2,1,0:T(8,128)}), f32[1,80,4096]{2,1,0:T(8,128)}) %reduce-scatter.19.cloned.1.call-update) | async-done | bytes 1310736
  815.8 109.3 %reduce-scatter.21.cloned.1.call-done = f32[1,80,4096]{2,1,0:T(8,128)} async-done(((f32[1,640,4096]{2,1,0:T(8,128)}), f32[1,80,4096]{2,1,0:T(8,128)}) %reduce-scatter.21.cloned.1.call-update) | async-done | bytes 1310736
  926.5 6.3 fusion.144
  932.8 91.5 %all-gather.14.cloned.1.call-done = bf16[1,2,4096,640]{3,2,1,0:T(8,128)(2,1)} async-done(((bf16[1,2,512,640]{3,2,1,0:T(8,128)(2,1)}), bf16[1,2,4096,640]{3,2,1,0:T(8,128)(2,1)}) %all-gather.14.cloned.1.call-update) | async-done | bytes 10485776 | tf_op jit(solution)/reshape | solution.py:52
  1024.3 99.9 %all-gather.12.cloned.1.call-done = bf16[1,2,640,4096]{3,2,1,0:T(8,128)(2,1)} async-done(((bf16[1,2,80,4096]{3,2,1,0:T(8,128)(2,1)}), bf16[1,2,640,4096]{3,2,1,0:T(8,128)(2,1)}) %all-gather.12.cloned.1.call-update) | async-done | bytes 10485776 | tf_op jit(solution)/reshape | solution.py:52
  1124.2 99.9 %all-gather.10.cloned.1.call-done = bf16[1,2,640,4096]{3,2,1,0:T(8,128)(2,1)} async-done(((bf16[1,2,80,4096]{3,2,1,0:T(8,128)(2,1)}), bf16[1,2,640,4096]{3,2,1,0:T(8,128)(2,1)}) %all-gather.10.cloned.1.call-update) | async-done | bytes 10485776 | tf_op jit(solution)/reshape | solution.py:52
  1224.2 9.7 copy.5
  1233.9 9.7 copy.6
  1243.6 9.0 copy.7
  (71 shorter events, 28.2 us)
Async XLA Ops:
  7.2 6.9 copy-start
  7.2 411.8 %reduce-scatter.29.cloned.1.call-start = ((), (), s32[]{:S(2)}) async-start(), calls=%async_computation.14 | async-start | bytes 11796480
  14.1 19.9 %copy-start.16 = (f32[2048]{0:T(1024)}, f32[2048]{0:T(1024)S(1)}, u32[]{:S(2)}) copy-start(f32[2048]{0:T(1024)S(1)} %add_rsqrt_fusion) | copy-start | bytes 24580
  98.3 20.7 %copy-start.1 = (bf16[1,1,2048,640]{2,3,1,0:T(8,128)(2,1)}, bf16[1,1,2048,640]{2,3,1,0:T(8,128)(2,1)S(1)}, u32[]{:S(2)}) copy-start(bf16[1,1,2048,640]{2,3,1,0:T(8,128)(2,1)S(1)} %get-tuple-element.10) | copy-start | bytes 7864324
  98.3 0.7 copy-start.11
  99.0 20.0 %copy-start.13 = (f32[1,1,2048]{2,1,0:T(1,128)}, f32[1,1,2048]{2,1,0:T(1,128)S(1)}, u32[]{:S(2)}) copy-start(f32[1,1,2048]{2,1,0:T(1,128)S(1)} %rsqrt.31) | copy-start | bytes 24580
  194.4 17.3 %copy-start.2 = (bf16[1,1,2048,640]{2,3,1,0:T(8,128)(2,1)S(1)}, bf16[1,1,2048,640]{2,3,1,0:T(8,128)(2,1)}, u32[]{:S(2)}) copy-start(bf16[1,1,2048,640]{2,3,1,0:T(8,128)(2,1)} %copy-done.1) | copy-start | bytes 7864324
  211.7 24.8 %copy-start.12 = (f32[2048]{0:T(1024)S(1)}, f32[2048]{0:T(1024)}, u32[]{:S(2)}) copy-start(f32[2048]{0:T(1024)} %copy-done.11) | copy-start | bytes 24580
  211.7 24.8 %copy-start.14 = (f32[1,1,2048]{2,1,0:T(1,128)S(1)}, f32[1,1,2048]{2,1,0:T(1,128)}, u32[]{:S(2)}) copy-start(f32[1,1,2048]{2,1,0:T(1,128)} %copy-done.13) | copy-start | bytes 24580
  240.1 1.5 copy-start.4
  260.6 1.7 copy-start.6
  260.6 222.3 %reduce-scatter.27.cloned.1.call-start = ((), (), s32[]{:S(2)}) async-start(), calls=%async_computation.13 | async-start | bytes 11796480
  291.1 1.7 copy-start.5
  291.1 20.3 %copy-start.17 = (f32[2048]{0:T(1024)S(1)}, f32[2048]{0:T(1024)}, u32[]{:S(2)}) copy-start(f32[2048]{0:T(1024)} %copy-done.16) | copy-start | bytes 24580
  291.1 302.6 %reduce-scatter.25.cloned.1.call-start = ((), (), s32[]{:S(2)}) async-start(), calls=%async_computation.12 | async-start | bytes 11796480
  337.0 1.7 copy-start.3
  337.0 1.7 copy-start.15
  337.1 366.7 %reduce-scatter.23.cloned.1.call-start = ((), (), s32[]{:S(2)}) async-start(), calls=%async_computation.11 | async-start | bytes 11796480
  363.9 450.5 %reduce-scatter.19.cloned.1.call-start = ((), (), s32[]{:S(2)}) async-start(), calls=%async_computation.9 | async-start | bytes 11796480
  380.9 1.7 copy-start.7
  380.9 544.2 %reduce-scatter.21.cloned.1.call-start = ((), (), s32[]{:S(2)}) async-start(), calls=%async_computation.10 | async-start | bytes 11796480
  417.0 0.7 copy-start.18
  417.0 67.3 %copy-start.8 = (f32[2,512,640]{2,1,0:T(8,128)S(1)}, f32[2,512,640]{2,1,0:T(8,128)}, u32[]{:S(2)}) copy-start(f32[2,512,640]{2,1,0:T(8,128)} %param.10) | copy-start | bytes 7864324
  417.1 607.3 %all-gather.14.cloned.1.call-start = ((), (), s32[]{:S(2)}) async-start(), calls=%async_computation.8 | async-start | bytes 11796480 | tf_op jit(solution)/reshape | solution.py:52
  490.6 214.5 %copy-start.9 = (f32[2,80,4096]{2,1,0:T(8,128)S(1)}, f32[2,80,4096]{2,1,0:T(8,128)}, u32[]{:S(2)}) copy-start(f32[2,80,4096]{2,1,0:T(8,128)} %param.8) | copy-start | bytes 7864324
  490.7 633.6 %all-gather.12.cloned.1.call-start = ((), (), s32[]{:S(2)}) async-start(), calls=%async_computation.7 | async-start | bytes 11796480 | tf_op jit(solution)/reshape | solution.py:52
  711.5 215.0 %copy-start.10 = (f32[2,80,4096]{2,1,0:T(8,128)S(1)}, f32[2,80,4096]{2,1,0:T(8,128)}, u32[]{:S(2)}) copy-start(f32[2,80,4096]{2,1,0:T(8,128)} %param.6) | copy-start | bytes 7864324
  711.5 512.6 %all-gather.10.cloned.1.call-start = ((), (), s32[]{:S(2)}) async-start(), calls=%async_computation.6 | async-start | bytes 11796480 | tf_op jit(solution)/reshape | solution.py:52
Sparse Core Ops, SparseCore 0:
  260.8 111.8 reduce-scatter.28
  375.0 107.8 reduce-scatter.26
  485.8 107.8 reduce-scatter.24
  595.9 107.8 reduce-scatter.22
  706.5 107.8 reduce-scatter.18
  817.2 107.8 reduce-scatter.20
  926.7 97.6 all-gather.13
  1026.5 97.6 all-gather.11
  1126.4 97.6 all-gather.9
where the time goes:
time: 1270 us; the launch traced here: 1260 us
  waiting for transfers between devices  778 us (61%)
  matrix products  326 us (26%)
  other arithmetic  93.9 us (7%)
  local copies, waits for them, and re-layouts  45.8 us (4%)
  between operations  15.2 us (1%)
    unnamed x15, waiting for transfers between devices  486 us
    reshape x3, waiting for transfers between devices, step(): t.reshape(-1, *t.shape[2:])  291 us
    dot_general x5, matrix products, layer(): up = jnp.dot(a, w['w_up'], preferred_element_type=jnp.float32)  115 us
    dot_general x5, matrix products, layer(): gate = jnp.dot(a, w['w_gate'], preferred_element_type=jnp.float32)  109 us
    dot_general x5, matrix products, matmul(): jnp.dot(a, w, preferred_element_type=jnp.float32).astype(jnp.bfloat16)  103 us
    unnamed x3, other arithmetic  64.2 us
    unnamed x43, local copies, waits for them, and re-layouts  45.2 us
  transfers between devices with their start and end apart: 9, of which 8 were waited for; matrix products, arithmetic and copies ran while one was open for 14% of the time, Pallas kernels for 0%

commit v1 on v0

v1 whole, which is shorter than its diff:
```python
import functools

import jax
import jax.numpy as jnp
from jax import lax
from jax.experimental import pallas as pl
from jax.experimental.pallas import tpu as pltpu
from jax.sharding import PartitionSpec as P

NAMES = ("w_gate", "w_up", "w_down")
MESH = pl.DeviceIdType.MESH

ROUNDS, MR = 96, 160
D0, LAG, LAGA, LAGD = 2, 2, 2, 2
RING, SLOTS = 16, 4
TICKS = ROUNDS + D0 + 3 * LAG + 3 * LAGA + max(LAGD, SLOTS)


def matmul(a, w):
    return jnp.dot(a, w, preferred_element_type=jnp.float32).astype(jnp.bfloat16)


def normed(h):
    wide = h.astype(jnp.float32)
    scale = lax.rsqrt(jnp.mean(wide**2, -1, keepdims=True) + 1e-6)
    return (wide * scale).astype(jnp.bfloat16)


def layer(h, w):
    a = normed(h)
    gate = jnp.dot(a, w["w_gate"], preferred_element_type=jnp.float32)
    up = jnp.dot(a, w["w_up"], preferred_element_type=jnp.float32)
    return h + matmul((jax.nn.silu(gate) * up).astype(jnp.bfloat16), w["w_down"])


def stack(weights, h):
    for number in range(weights["w_gate"].shape[0]):
        h = layer(h, {name: w[number] for name, w in weights.items()})
    return h


def within(r):
    return (r >= 0) & (r < ROUNDS)


def kernel(
    terms, w_g, w_u, w_d, m_g, m_u, m_d, v_g, v_u, v_d,
    news, grads, partner_terms, line_terms,
    fetched, summed, fresh, final, wb, mb, vb, wdb, mdb, vdb,
    sem_pair_s, sem_pair_r, sem_line_s, sem_line_r, sem_fetch, sem_state, sem_own, sem_ag_s, sem_ag_r, sem_agp_s, sem_agp_r,
):
    me = lax.axis_index("dp")
    z, c = lax.div(me, 2), lax.rem(me, 2)
    partner = me + 1 - 2 * c

    barrier = pltpu.get_barrier_semaphore()
    pl.semaphore_signal(barrier, inc=1, device_id={"dp": partner}, device_id_type=MESH)

    @pl.when(z > 0)
    def _():
        pl.semaphore_signal(barrier, inc=1, device_id={"dp": me - 2}, device_id_type=MESH)

    @pl.when(z < 3)
    def _():
        pl.semaphore_signal(barrier, inc=1, device_id={"dp": me + 2}, device_id_type=MESH)

    pl.semaphore_wait(barrier, 1 + (z > 0).astype(jnp.int32) + (z < 3).astype(jnp.int32))
    fetched[...] = jnp.zeros_like(fetched)

    def remote(src, dst, send, recv, dev):
        return pltpu.make_async_remote_copy(src, dst, send, recv, device_id={"dp": dev}, device_id_type=MESH)

    def pair(r):
        return remote(terms.at[r, 1 - c], partner_terms.at[r], sem_pair_s.at[lax.rem(r, SLOTS)], sem_pair_r.at[lax.rem(r, RING)], partner)

    def most(zp):
        return jnp.maximum(zp, 3 - zp)

    def fetch(i, which, src):
        return pltpu.make_async_copy(src, fetched.at[i, which], sem_fetch.at[i, which])

    class Line:
        def __init__(self, i, k):
            self.i, self.zp = i, lax.rem(z + 1 + i, 4)
            self.right = self.zp > z
            self.r = k - D0 - LAG * jnp.where(self.right, z, 3 - z)
            self.has_in = jnp.where(self.right, z > 0, z < 3)
            self.ok = within(self.r)

        def send(self, r):
            nxt = jnp.where(self.right, z + 1, z - 1)
            place = jnp.where((nxt == self.zp) & ~self.right, 4, self.zp)
            slot = lax.rem(r, SLOTS)
            return remote(
                summed.at[self.i, slot], line_terms.at[r, place],
                sem_line_s.at[self.i, slot], sem_line_r.at[place, lax.rem(r, RING)], 2 * nxt + c,
            )

        def arrival(self):
            return remote(
                summed.at[self.i, 0], line_terms.at[self.r, self.zp],
                sem_line_s.at[self.i, 0], sem_line_r.at[self.zp, lax.rem(self.r, RING)], partner,
            )

        def begin(self):
            @pl.when(self.ok)
            def _():
                fetch(self.i, 0, terms.at[self.r, c, self.zp]).start()
                fetch(self.i, 1, partner_terms.at[self.r, self.zp]).start()

            @pl.when(self.ok & self.has_in)
            def _():
                self.arrival().wait_recv()
                fetch(self.i, 2, line_terms.at[self.r, self.zp]).start()

        def finish(self):
            @pl.when(within(self.r - SLOTS))
            def _():
                self.send(self.r - SLOTS).wait_send()

            @pl.when(self.ok & self.has_in)
            def _():
                fetch(self.i, 2, line_terms.at[self.r, self.zp]).wait()

            @pl.when(self.ok)
            def _():
                fetch(self.i, 0, terms.at[self.r, c, self.zp]).wait()
                fetch(self.i, 1, partner_terms.at[self.r, self.zp]).wait()
                total = (
                    fetched[self.i, 0].astype(jnp.float32)
                    + fetched[self.i, 1].astype(jnp.float32)
                    + fetched[self.i, 2].astype(jnp.float32)
                )
                summed[self.i, lax.rem(self.r, SLOTS)] = total.astype(jnp.bfloat16)
                self.send(self.r).start()

    def state(r, go):
        kind, q, j = lax.rem(lax.div(r, 4), 3), lax.rem(r, 4), lax.rem(lax.div(r, 12), 4)
        of = 1 - lax.div(r, 48)

        @pl.when(kind == 0)
        def _():
            mine = pl.multiple_of(128 * j + 32 * q, 32)
            row = pl.multiple_of(512 * me + 128 * j + 32 * q, 32)
            go(pltpu.make_async_copy(w_d.at[of, pl.ds(row, 32)], wdb, sem_state.at[0, 0]))
            go(pltpu.make_async_copy(m_d.at[of, pl.ds(mine, 32)], mdb, sem_state.at[1, 0]))
            go(pltpu.make_async_copy(v_d.at[of, pl.ds(mine, 32)], vdb, sem_state.at[2, 0]))

        for number, (w, m, v) in ((1, (w_g, m_g, v_g)), (2, (w_u, m_u, v_u))):

            @pl.when(kind == number)
            def _(w=w, m=m, v=v):
                row = pl.multiple_of(80 * me, 16)
                for s in range(2):
                    col = pl.multiple_of(512 * (2 * q + s) + 128 * j, 128)
                    to = pl.ds(80 * s, 80)
                    go(pltpu.make_async_copy(w.at[of, pl.ds(row, 80), pl.ds(col, 128)], wb.at[to], sem_state.at[0, s]))
                    go(pltpu.make_async_copy(m.at[of, :, pl.ds(col, 128)], mb.at[to], sem_state.at[1, s]))
                    go(pltpu.make_async_copy(v.at[of, :, pl.ds(col, 128)], vb.at[to], sem_state.at[2, s]))

    def adamw(w, m, v, g):
        g = g.astype(jnp.float32)
        m = 0.9 * m + 0.1 * g
        v = 0.95 * v + 0.05 * g * g
        return (w - 0.02 * (m * lax.rsqrt(v + 1e-8) + 0.1 * w)).astype(jnp.bfloat16)

    class Own:
        def __init__(self, k):
            self.r = k - D0 - LAG * most(z)
            self.ok = within(self.r)

        def outs(self, r, go):
            slot, ring = lax.rem(r, SLOTS), lax.rem(r, RING)
            src, dst = fresh.at[slot], news.at[r, c, z]

            @pl.when(z < 3)
            def _():
                go(remote(src, dst, sem_own.at[0, slot], sem_ag_r.at[z, ring], me + 2))

            @pl.when(z > 0)
            def _():
                go(remote(src, dst, sem_own.at[1, slot], sem_ag_r.at[z, ring], me - 2))

            go(remote(src, dst, sem_own.at[2, slot], sem_agp_r.at[z, ring], partner))

        def local(self, r, go):
            slot = lax.rem(r, SLOTS)
            go(pltpu.make_async_copy(fresh.at[slot], news.at[r, c, z], sem_own.at[3, slot]))
            go(pltpu.make_async_copy(final.at[slot], grads.at[r], sem_own.at[4, slot]))

        def arrival(self, place):
            return remote(
                summed.at[0, 0], line_terms.at[self.r, place],
                sem_line_s.at[0, 0], sem_line_r.at[place, lax.rem(self.r, RING)], partner,
            )

        def begin(self):
            @pl.when(self.ok)
            def _():
                fetch(3, 0, terms.at[self.r, c, z]).start()
                fetch(3, 1, partner_terms.at[self.r, z]).start()
                state(self.r, lambda d: d.start())

            @pl.when(self.ok & (z > 0))
            def _():
                self.arrival(z).wait_recv()
                fetch(3, 2, line_terms.at[self.r, z]).start()

            @pl.when(self.ok & (z < 3))
            def _():
                self.arrival(4).wait_recv()
                fetch(3, 3, line_terms.at[self.r, 4]).start()

        def finish(self):
            @pl.when(within(self.r - SLOTS))
            def _():
                self.outs(self.r - SLOTS, lambda d: d.wait_send())
                self.local(self.r - SLOTS, lambda d: d.wait())

            @pl.when(self.ok & (z > 0))
            def _():
                fetch(3, 2, line_terms.at[self.r, z]).wait()

            @pl.when(self.ok & (z < 3))
            def _():
                fetch(3, 3, line_terms.at[self.r, 4]).wait()

            @pl.when(self.ok)
            def _():
                slot = lax.rem(self.r, SLOTS)
                kind = lax.rem(lax.div(self.r, 4), 3)
                fetch(3, 0, terms.at[self.r, c, z]).wait()
                fetch(3, 1, partner_terms.at[self.r, z]).wait()
                state(self.r, lambda d: d.wait())
                total = fetched[3, 0].astype(jnp.float32) + fetched[3, 1].astype(jnp.float32)
                total = total + fetched[3, 2].astype(jnp.float32) + fetched[3, 3].astype(jnp.float32)
                final[slot] = total.astype(jnp.bfloat16)

                @pl.when(kind == 0)
                def _():
                    for i in range(5):
                        rows, cols = pl.ds(32 * i, 32), pl.ds(128 * i, 128)
                        w = wdb[:, cols].astype(jnp.float32)
                        fresh[slot, rows] = adamw(w, mdb[:, cols], vdb[:, cols], final[slot, rows])

                @pl.when(kind != 0)
                def _():
                    fresh[slot] = adamw(wb[...].astype(jnp.float32), mb[...], vb[...], final[slot])

                self.outs(self.r, lambda d: d.start())
                self.local(self.r, lambda d: d.start())

    class Gather:
        def __init__(self, i, k):
            self.i, self.zp = i, lax.rem(z + 1 + i, 4)
            self.r = k - D0 - LAG * most(self.zp) - LAGA * jnp.abs(z - self.zp)
            self.on = jnp.where(self.zp < z, z < 3, z > 0)

        def forward(self, r):
            nxt = jnp.where(self.zp < z, z + 1, z - 1)
            at = news.at[r, c, self.zp]
            return remote(at, at, sem_ag_s.at[self.i, lax.rem(r, SLOTS)], sem_ag_r.at[self.zp, lax.rem(r, RING)], 2 * nxt + c)

        def across(self, r):
            at = news.at[r, c, self.zp]
            return remote(at, at, sem_agp_s.at[self.i, lax.rem(r, SLOTS)], sem_agp_r.at[self.zp, lax.rem(r, RING)], partner)

        def step(self):
            @pl.when(within(self.r - SLOTS) & self.on)
            def _():
                self.forward(self.r - SLOTS).wait_send()

            @pl.when(within(self.r - SLOTS))
            def _():
                self.across(self.r - SLOTS).wait_send()

            @pl.when(within(self.r))
            def _():
                self.forward(self.r).wait_recv()

            @pl.when(within(self.r) & self.on)
            def _():
                self.forward(self.r).start()

            @pl.when(within(self.r))
            def _():
                self.across(self.r).start()

    def tick(k, work=None):
        @pl.when(within(k - SLOTS))
        def _():
            pair(k - SLOTS).wait_send()

        @pl.when(within(k))
        def _():
            pair(k).start()

        @pl.when(within(k - D0))
        def _():
            pair(k - D0).wait_recv()

        own, lines = Own(k), [Line(i, k) for i in range(3)]
        for line in lines:
            line.begin()
        own.begin()
        for i in range(3):
            Gather(i, k).step()
        for zp in range(4):
            r = k - D0 - LAG * most(zp) - LAGA * jnp.abs(z - zp) - LAGD

            @pl.when(within(r))
            def _(r=r, zp=zp):
                at = news.at[r, 1 - c, zp]
                remote(at, at, sem_agp_s.at[0, 0], sem_agp_r.at[zp, lax.rem(r, RING)], partner).wait_recv()

        if work is not None:
            work()
        for line in lines:
            line.finish()
        own.finish()

    @pl.loop(0, TICKS)
    def _(k):
        tick(k)


def exchange(terms, weights, m, v):
    bf, f32, dma = jnp.bfloat16, jnp.float32, pltpu.SemaphoreType.DMA
    message = (MR, 128)
    return pl.pallas_call(
        kernel,
        name="exchange",
        out_shape=(
            jax.ShapeDtypeStruct((ROUNDS, 2, 4, *message), bf),
            jax.ShapeDtypeStruct((ROUNDS, *message), bf),
            jax.ShapeDtypeStruct((ROUNDS, 4, *message), bf),
            jax.ShapeDtypeStruct((ROUNDS, 5, *message), bf),
        ),
        in_specs=[pl.BlockSpec(memory_space=pl.ANY)] * 10,
        out_specs=[pl.BlockSpec(memory_space=pl.ANY)] * 4,
        scratch_shapes=[
            pltpu.VMEM((4, 4, *message), bf),
            pltpu.VMEM((3, SLOTS, *message), bf),
            pltpu.VMEM((SLOTS, *message), bf),
            pltpu.VMEM((SLOTS, *message), bf),
            pltpu.VMEM(message, bf), pltpu.VMEM(message, f32), pltpu.VMEM(message, f32),
            pltpu.VMEM((32, 640), bf), pltpu.VMEM((32, 640), f32), pltpu.VMEM((32, 640), f32),
            dma((SLOTS,)), dma((RING,)), dma((3, SLOTS)), dma((5, RING)), dma((4, 4)), dma((3, 2)), dma((5, SLOTS)),
            dma((3, SLOTS)), dma((4, RING)), dma((3, SLOTS)), dma((4, RING)),
        ],
        compiler_params=pltpu.CompilerParams(collective_id=0, has_side_effects=True, vmem_limit_bytes=60 * 2**20),
    )(terms, *weights, *m, *v)


def to_messages(gate, up, down):
    def wide(g):
        g = g.reshape(2, 8, 80, 4, 2, 4, 128)[::-1]
        return g.transpose(0, 5, 3, 1, 4, 2, 6).reshape(2, 4, 1, 4, 8, MR, 128)

    d = down.reshape(2, 8, 4, 4, 32, 5, 128)[::-1].transpose(0, 2, 3, 1, 5, 4, 6).reshape(2, 4, 1, 4, 8, MR, 128)
    g = jnp.concatenate([d, wide(gate), wide(up)], axis=2).reshape(ROUNDS, 4, 2, MR, 128)
    return g.transpose(0, 2, 1, 3, 4)


def from_messages(w, owners):
    w = w.reshape(2, 4, 3, 4, owners, MR, 128)[::-1]

    def wide(x):
        return x.reshape(2, 4, 4, owners, 2, 80, 128).transpose(0, 3, 5, 2, 4, 1, 6).reshape(2, owners * 80, 4096)

    down = w[:, :, 0].reshape(2, 4, 4, owners, 5, 32, 128).transpose(0, 3, 1, 2, 5, 4, 6).reshape(2, owners * 512, 640)
    return wide(w[:, :, 1]), wide(w[:, :, 2]), down


def solution(mesh):
    def step(x, dy, *arrays):
        weights, m, v = (arrays[i : i + 3] for i in (0, 3, 6))
        _, back = jax.vjp(lambda w: stack(w, x[0]), dict(zip(NAMES, weights, strict=True)))
        by_weights = back(dy[0])[0]
        terms = to_messages(*(by_weights[name] for name in NAMES))
        news, grads, _, _ = exchange(terms, weights, m, v)
        fresh = from_messages(news.transpose(0, 2, 1, 3, 4).reshape(ROUNDS, 8, MR, 128), 8)
        g = [t.astype(jnp.float32) for t in from_messages(grads, 1)]
        m = [0.9 * a + 0.1 * b for a, b in zip(m, g, strict=True)]
        v = [0.95 * a + 0.05 * b * b for a, b in zip(v, g, strict=True)]
        return (*fresh, *m, *v)

    whole, rows = P(None, None, None), P(None, "dp", None)
    return jax.shard_map(
        step,
        mesh=mesh,
        in_specs=(P(("rep", "dp"), None, None),) * 2 + (whole,) * 3 + (rows,) * 6,
        out_specs=(P("rep", None, None),) * 3 + (P("rep", "dp", None),) * 6,
        check_vma=False,
    )
```

time: 1270 us -> 1200 us (0.945)
  waiting for transfers between devices: 778 us -> 0 us
  Pallas kernels: 0 us -> 366 us
  local copies, waits for them, and re-layouts: 45.8 us -> 388 us
  matrix products: 326 us -> 356 us
  other arithmetic: 93.9 us -> 70.2 us
  between operations: 15.2 us -> 1.03 us
    unnamed x15 -> x0, waiting for transfers between devices: 486 us -> none
    pallas_call x0 -> x1, Pallas kernels: none -> 366 us  [exchange(): pl.pallas_call(kernel, name='exchange', out_shape=(jax.ShapeDtypeStruct((...]
    reshape x3 -> x0, waiting for transfers between devices: 291 us -> none  [step(): t.reshape(-1, *t.shape[2:])]
    reshape x0 -> x9, local copies, waits for them, and re-layouts: none -> 165 us  [the longest x4 59.7 us: wide(): g = g.reshape(2, 8, 80, 4, 2, 4, 128)[::-1]]
    transpose x0 -> x6, local copies, waits for them, and re-layouts: none -> 83.8 us  [the longest x2 29.4 us: wide(): x.reshape(2, 4, 4, owners, 2, 80, 128).transpose(0, 3, 5, 2, 4, 1, 6)]
    unnamed x3 -> x1, other arithmetic: 64.2 us -> 0.01 us
    slice x0 -> x7, local copies, waits for them, and re-layouts: none -> 62.8 us  [the longest x3 37.3 us: from_messages(): w[:, :, 0].reshape(2, 4, 4, owners, 5, 32, 128)]
    unnamed x43 -> x35, local copies, waits for them, and re-layouts: 45.2 us -> 11.5 us
  transfers between devices with their start and end apart: 9 -> 0, of which waited for: 8 -> 0; matrix products, arithmetic and copies ran while one was open for 14% -> 0% of each run, Pallas kernels for 0% -> 0%
where the time goes in v1:
time: 1200 us; the launch traced here: 1180 us
  local copies, waits for them, and re-layouts  388 us (32%)
  Pallas kernels  366 us (30%)
  matrix products  356 us (30%)
  other arithmetic  70.2 us (6%)
    pallas_call x1, Pallas kernels, exchange(): pl.pallas_call(kernel, name='exchange', out_shape=(jax.ShapeDtypeStruct((...  366 us
    dot_general x5, matrix products, layer(): gate = jnp.dot(a, w['w_gate'], preferred_element_type=jnp.float32)  129 us
    dot_general x5, matrix products, layer(): up = jnp.dot(a, w['w_up'], preferred_element_type=jnp.float32)  123 us
    dot_general x5, matrix products, matmul(): jnp.dot(a, w, preferred_element_type=jnp.float32).astype(jnp.bfloat16)  105 us
    reshape x4, local copies, waits for them, and re-layouts, wide(): g = g.reshape(2, 8, 80, 4, 2, 4, 128)[::-1]  59.7 us
    slice x3, local copies, waits for them, and re-layouts, from_messages(): w[:, :, 0].reshape(2, 4, 4, owners, 5, 32, 128)  37.3 us
    reshape x2, local copies, waits for them, and re-layouts, wide(): x.reshape(2, 4, 4, owners, 2, 80, 128).transpose(0, 3, 5, 2, 4, 1, 6)  35.6 us
    transpose x2, local copies, waits for them, and re-layouts, wide(): x.reshape(2, 4, 4, owners, 2, 80, 128).transpose(0, 3, 5, 2, 4, 1, 6)  29.4 us

profile of v1, /device:TPU:0, one launch (start us, length us, event | category | flops | bytes accessed | tf_op | source)
XLA Modules:
  0.0 1180.6 jit_solution(2318300553086835459)
XLA Ops:
  4.2 22.4 %fusion.50 = f32[2048,4096]{1,0:T(8,128)} fusion(bf16[2,640,4096]{2,1,0:T(8,128)(2,1)} %w_g.1, bf16[1,2048,640]{2,1,0:T(8,128)(2,1)} %param.11, f32[2048]{0:T(1024)S(1)} %add_rsqrt_fusion), kind=kOutput, calls=%fused_computation.71 | convolution fusion | flops 10741350400 | bytes 41426944 | tf_op jit(solution)/shard_map/jvp()/dot_general | solution.py:31
  26.6 32.3 %multiply_convert_fusion.1 = (bf16[2048,4096]{1,0:T(8,128)(2,1)}, f32[2048,4096]{1,0:T(8,128)}) fusion(f32[2048,4096]{1,0:T(8,128)} %fusion.50, bf16[2,640,4096]{2,1,0:T(8,128)(2,1)} %w_u.1, bf16[1,2048,640]{2,1,0:T(8,128)(2,1)} %param.11, f32[2048]{0:T(1024)S(1)} %add_rsqrt_fusion), kind=kOutput, calls=%fused_computation.17 | convolution fusion | flops 10791682048 | bytes 91758592 | tf_op jit(solution)/shard_map/jvp()/dot_general | solution.py:32
  59.0 18.0 %fusion.34 = (f32[2048]{0:T(1024)S(1)}, bf16[2048,640]{0,1:T(8,128)(2,1)}) fusion(bf16[2048,4096]{1,0:T(8,128)(2,1)} %get-tuple-element.25, bf16[2,4096,640]{2,1,0:T(8,128)(2,1)} %w_d.1, bf16[1,2048,640]{1,2,0:T(8,128)(2,1)S(1)} %copy.36), kind=kOutput, calls=%fused_computation.55 | convolution fusion | flops 10743969792 | bytes 27271168 | tf_op jit(solution)/shard_map/jvp()/dot_general | solution.py:20
  77.0 22.3 %fusion.39 = f32[2048,4096]{1,0:T(8,128)} fusion(bf16[2,640,4096]{2,1,0:T(8,128)(2,1)} %w_u.1, bf16[2048,640]{0,1:T(8,128)(2,1)} %get-tuple-element.28, f32[2048]{0:T(1024)S(1)} %fusion.91), kind=kOutput, calls=%fused_computation.60 | convolution fusion | flops 10741350400 | bytes 41426944 | tf_op jit(solution)/shard_map/jvp()/dot_general | solution.py:32
  99.3 19.7 %convolution_convert_fusion.1 = bf16[2048,4096]{1,0:T(8,128)(2,1)} fusion(bf16[2,4096,640]{2,1,0:T(8,128)(2,1)} %w_d.1, bf16[1,2048,640]{2,1,0:T(8,128)(2,1)} %param.12), kind=kOutput, calls=%fused_computation.28 | convolution fusion | flops 10745806848 | bytes 24641536 | tf_op jit(solution)/shard_map/transpose(jvp())/dot_general | solution.py:20
  119.0 42.6 %fusion.2 = (bf16[2048,4096]{1,0:T(8,128)(2,1)}, f32[2048,4096]{1,0:T(8,128)}) fusion(f32[2048,4096]{1,0:T(8,128)} %fusion.39, bf16[2048,4096]{1,0:T(8,128)(2,1)} %convolution_convert_fusion.1, bf16[2,640,4096]{2,1,0:T(8,128)(2,1)} %w_g.1, bf16[2048,640]{0,1:T(8,128)(2,1)S(1)} %copy-done.5, f32[2048]{0:T(1024)S(1)} %fusion.91), kind=kOutput, calls=%fused_computation.8 | convolution fusion | flops 10842013696 | bytes 108535808 | tf_op jit(solution)/shard_map/jvp()/dot_general | solution.py:31
  161.6 28.4 %fusion.28 = bf16[1,4096,640]{2,1,0:T(8,128)(2,1)} fusion(f32[2048,4096]{1,0:T(8,128)} %fusion.39, bf16[1,2048,640]{2,1,0:T(8,128)(2,1)} %param.12, f32[2048,4096]{1,0:T(8,128)} %get-tuple-element.30), kind=kOutput, calls=%fused_computation.49 | convolution fusion | flops 10790371328 | bytes 74973184 | tf_op jit(solution)/shard_map/transpose(jvp())/dot_general | solution.py:20
  190.0 21.0 %fusion.64 = bf16[2048,640]{0,1:T(8,128)(2,1)S(1)} fusion(bf16[2,640,4096]{2,1,0:T(8,128)(2,1)} %w_u.1, bf16[2048,4096]{1,0:T(8,128)(2,1)} %convolution_convert_fusion.1, f32[2048,4096]{1,0:T(8,128)} %get-tuple-element.30), kind=kOutput, calls=%fused_computation.87 | convolution fusion | flops 10789060608 | bytes 58195968 | tf_op jit(solution)/shard_map/transpose(jvp())/dot_general | solution.py:32
  211.0 17.4 %fusion.36 = (f32[2048]{0:T(1024)S(1)}, bf16[2048,640]{0,1:T(8,128)(2,1)}) fusion(bf16[2048,640]{0,1:T(8,128)(2,1)S(1)} %copy-done.5, bf16[2048,640]{0,1:T(8,128)(2,1)S(1)} %fusion.64, bf16[2048,4096]{1,0:T(8,128)(2,1)} %get-tuple-element.29, bf16[2,640,4096]{2,1,0:T(8,128)(2,1)} %w_g.1), kind=kOutput, calls=%fused_computation.57 | convolution fusion | flops 10743969792 | bytes 29892608 | tf_op jit(solution)/shard_map/transpose(jvp())/dot_general | solution.py:31
  237.2 19.1 %fusion.29 = bf16[1,4096,640]{2,1,0:T(8,128)(2,1)} fusion(bf16[2048,4096]{1,0:T(8,128)(2,1)} %get-tuple-element.25, bf16[2048,640]{0,1:T(8,128)(2,1)S(1)} %fusion.80), kind=kOutput, calls=%fused_computation.50 | convolution fusion | flops 10740039680 | bytes 24641536 | tf_op jit(solution)/shard_map/transpose(jvp())/dot_general | solution.py:20
  265.3 23.5 %reshape.106 = bf16[2,8,4,4,32,5,128]{6,5,4,3,2,1,0:T(8,128)(2,1)} reshape(bf16[2,4096,640]{2,1,0:T(8,128)(2,1)} %pad_add_fusion.2) | data formatting | bytes 20971520 | tf_op jit(solution)/shard_map/reshape | solution.py:360
  306.8 12.9 %fusion.22 = bf16[1,640,4096]{2,1,0:T(8,128)(2,1)} fusion(bf16[2048,4096]{1,0:T(8,128)(2,1)S(1)} %bitcast.144, bf16[2048,640]{0,1:T(8,128)(2,1)S(1)} %copy-done.6, f32[2048]{0:T(1024)S(1)} %fusion.91), kind=kOutput, calls=%fused_computation.45 | convolution fusion | flops 10741350400 | bytes 24649728 | tf_op jit(solution)/shard_map/transpose(jvp())/dot_general | solution.py:31
  319.7 19.7 %convolution_convert_fusion = bf16[2048,4096]{1,0:T(8,128)(2,1)} fusion(bf16[2048,640]{0,1:T(8,128)(2,1)} %copy-done.7, bf16[2,4096,640]{2,1,0:T(8,128)(2,1)} %w_d.1), kind=kOutput, calls=%fused_computation.27 | convolution fusion | flops 10745806848 | bytes 24641536 | tf_op jit(solution)/shard_map/transpose(jvp())/dot_general | solution.py:20
  339.4 33.2 %fusion.24 = bf16[1,640,4096]{2,1,0:T(8,128)(2,1)} fusion(f32[2048,4096]{1,0:T(8,128)} %fusion.50, f32[2048,4096]{1,0:T(8,128)} %get-tuple-element.26, bf16[2048,4096]{1,0:T(8,128)(2,1)} %convolution_convert_fusion, bf16[1,2048,640]{1,2,0:T(8,128)(2,1)S(1)} %copy-done.3, f32[2048]{0:T(1024)S(1)} %copy-done.11), kind=kOutput, calls=%fused_computation.47 | convolution fusion | flops 10836246528 | bytes 91758592 | tf_op jit(solution)/shard_map/transpose(jvp())/dot_general | solution.py:31
  381.4 18.0 %reshape.108 = bf16[2,8,80,4,2,4,128]{6,5,4,3,2,1,0:T(4,128)(2,1)} reshape(bf16[2,640,4096]{2,1,0:T(8,128)(2,1)} %pad_add_fusion.1) | data formatting | bytes 20971520 | tf_op jit(solution)/shard_map/reshape | solution.py:357
  399.4 12.1 %copy.39 = bf16[2,8,80,4,2,4,128]{6,2,4,1,3,5,0:T(8,128)(2,1)} copy(bf16[2,8,80,4,2,4,128]{6,5,4,3,2,1,0:T(4,128)(2,1)} %reshape.108) | data formatting | bytes 20971520 | tf_op jit(solution)/shard_map/reshape | solution.py:357
  422.5 23.8 %fusion.27 = bf16[1,640,4096]{2,1,0:T(8,128)(2,1)} fusion(bf16[2048,4096]{1,0:T(8,128)(2,1)} %convolution_convert_fusion.1, bf16[2048,640]{0,1:T(8,128)(2,1)} %get-tuple-element.28, f32[2048]{0:T(1024)S(1)} %fusion.91, f32[2048,4096]{1,0:T(8,128)} %get-tuple-element.30), kind=kOutput, calls=%fused_computation.48 | convolution fusion | flops 10794303488 | bytes 58204160 | tf_op jit(solution)/shard_map/transpose(jvp())/dot_general | solution.py:32
  446.3 23.1 %fusion.23 = bf16[1,640,4096]{2,1,0:T(8,128)(2,1)} fusion(bf16[2048,4096]{1,0:T(8,128)(2,1)} %convolution_convert_fusion, f32[2048,4096]{1,0:T(8,128)} %fusion.50, bf16[1,2048,640]{1,2,0:T(8,128)(2,1)S(1)} %copy-done.3, f32[2048]{0:T(1024)S(1)} %copy-done.11), kind=kOutput, calls=%fused_computation.46 | convolution fusion | flops 10794303488 | bytes 58204160 | tf_op jit(solution)/shard_map/transpose(jvp())/dot_general | solution.py:32
  478.2 17.5 %reshape.110 = bf16[2,8,80,4,2,4,128]{6,5,4,3,2,1,0:T(4,128)(2,1)} reshape(bf16[2,640,4096]{2,1,0:T(8,128)(2,1)} %pad_add_fusion) | data formatting | bytes 20971520 | tf_op jit(solution)/shard_map/reshape | solution.py:357
  495.7 12.1 %copy.40 = bf16[2,8,80,4,2,4,128]{6,2,4,1,3,5,0:T(8,128)(2,1)} copy(bf16[2,8,80,4,2,4,128]{6,5,4,3,2,1,0:T(4,128)(2,1)} %reshape.110) | data formatting | bytes 20971520 | tf_op jit(solution)/shard_map/reshape | solution.py:357
  518.8 21.9 %pad_maximum_fusion = bf16[2,4,3,4,8,160,128]{6,5,4,3,1,0,2:T(8,128)(2,1)} fusion(bf16[2,4,1,4,8,160,128]{6,5,4,3,1,0,2:T(8,128)(2,1)} %bitcast.135, bf16[2,4,1,4,8,160,128]{6,5,4,3,1,0,2:T(8,128)(2,1)} %bitcast.134, bf16[2,4,1,4,8,160,128]{6,5,4,3,1,0,2:T(8,128)(2,1)} %bitcast.133), kind=kLoop, calls=%fused_computation.20 | loop fusion | flops 31457280 | bytes 62914560 | tf_op jit(solution)/shard_map/concatenate | solution.py:361
  540.7 21.7 %copy.41 = bf16[2,4,3,4,8,160,128]{6,5,4,3,2,1,0:T(8,128)(2,1)} copy(bf16[2,4,3,4,8,160,128]{6,5,4,3,1,0,2:T(8,128)(2,1)} %pad_maximum_fusion) | data formatting | bytes 62914560 | tf_op jit(solution)/shard_map/concatenate | solution.py:361
  562.4 21.8 %copy.55 = bf16[96,4,2,160,128]{4,3,1,2,0:T(8,128)(2,1)} copy(bf16[96,4,2,160,128]{4,3,2,1,0:T(8,128)(2,1)} %bitcast.129) | data formatting | bytes 62914560 | tf_op jit(solution)/shard_map/reshape | solution.py:361
  584.2 365.6 %exchange.1 = (bf16[96,2,4,160,128]{4,3,2,1,0:T(8,128)(2,1)}, bf16[96,160,128]{2,1,0:T(8,128)(2,1)}, bf16[96,4,160,128]{3,2,1,0:T(8,128)(2,1)}, bf16[96,5,160,128]{3,2,1,0:T(8,128)(2,1)}) custom-call(bf16[96,2,4,160,128]{4,3,2,1,0:T(8,128)(2,1)} %bitcast.127, bf16[2,640,4096]{2,1,0:T(8,128)(2,1)} %w_g.1, bf16[2,640,4096]{2,1,0:T(8,128)(2,1)} %w_u.1, ...), custom_call_target="tpu_custom_call" | custom-call | tf_op jit(solution)/shard_map/exchange/pallas_call | solution.py:330
  980.7 22.1 %copy.43 = bf16[96,4,2,160,128]{4,3,2,1,0:T(8,128)(2,1)} copy(bf16[96,4,2,160,128]{4,3,1,2,0:T(8,128)(2,1)} %bitcast.136) | data formatting | bytes 62914560 | tf_op jit(solution)/shard_map/transpose | solution.py:382
  1002.8 26.3 %fusion.97 = (bf16[2,4,1,4,8,160,128]{6,5,4,3,2,1,0:T(8,128)(2,1)}, bf16[2,4,1,4,8,160,128]{6,5,4,3,2,1,0:T(8,128)(2,1)}, bf16[2,4,1,4,8,160,128]{6,5,4,3,2,1,0:T(8,128)(2,1)}) fusion(bf16[2,4,3,4,8,160,128]{6,5,4,3,2,1,0:T(8,128)(2,1)} %bitcast.128), kind=kLoop, calls=%fused_computation.111 | loop fusion | bytes 62914560 | tf_op jit(solution)/shard_map/slice | solution.py:371
  1040.0 14.4 %copy.46 = bf16[2,8,4,4,32,5,128]{6,5,4,3,2,1,0:T(8,128)(2,1)} copy(bf16[2,8,4,4,32,5,128]{6,4,5,1,3,2,0:T(8,128)(2,1)} %bitcast.130) | data formatting | bytes 20971520 | tf_op jit(solution)/shard_map/transpose | solution.py:371
  1054.4 24.3 %reshape.115 = bf16[2,4096,640]{2,1,0:T(8,128)(2,1)} reshape(bf16[2,8,4,4,32,5,128]{6,5,4,3,2,1,0:T(8,128)(2,1)} %copy.46) | data formatting | bytes 20971520 | tf_op jit(solution)/shard_map/reshape | solution.py:371
  1089.6 14.7 %copy.44 = bf16[2,8,80,4,2,4,128]{6,5,4,3,2,1,0:T(4,128)(2,1)} copy(bf16[2,8,80,4,2,4,128]{6,2,4,1,3,5,0:T(8,128)(2,1)} %bitcast.131) | data formatting | bytes 20971520 | tf_op jit(solution)/shard_map/transpose | solution.py:369
  1104.3 17.7 %reshape.113 = bf16[2,640,4096]{2,1,0:T(8,128)(2,1)} reshape(bf16[2,8,80,4,2,4,128]{6,5,4,3,2,1,0:T(4,128)(2,1)} %copy.44) | data formatting | bytes 20971520 | tf_op jit(solution)/shard_map/reshape | solution.py:369
  1132.9 14.7 %copy.45 = bf16[2,8,80,4,2,4,128]{6,5,4,3,2,1,0:T(4,128)(2,1)} copy(bf16[2,8,80,4,2,4,128]{6,2,4,1,3,5,0:T(8,128)(2,1)} %bitcast.132) | data formatting | bytes 20971520 | tf_op jit(solution)/shard_map/transpose | solution.py:369
  1147.6 17.8 %reshape.114 = bf16[2,640,4096]{2,1,0:T(8,128)(2,1)} reshape(bf16[2,8,80,4,2,4,128]{6,5,4,3,2,1,0:T(4,128)(2,1)} %copy.45) | data formatting | bytes 20971520 | tf_op jit(solution)/shard_map/reshape | solution.py:369
  (63 shorter events, 157.5 us)
Async XLA Ops:
  3.6 55.4 %copy-start.2 = (bf16[1,2048,640]{1,2,0:T(8,128)(2,1)}, bf16[1,2048,640]{1,2,0:T(8,128)(2,1)S(1)}, u32[]{:S(2)}) copy-start(bf16[1,2048,640]{1,2,0:T(8,128)(2,1)S(1)} %copy.36) | copy-start | bytes 7864324
  4.2 22.4 %copy-start.10 = (f32[2048]{0:T(1024)}, f32[2048]{0:T(1024)S(1)}, u32[]{:S(2)}) copy-start(f32[2048]{0:T(1024)S(1)} %add_rsqrt_fusion) | copy-start | bytes 24580
  77.0 22.3 %copy-start.8 = (f32[2048]{0:T(1024)}, f32[2048]{0:T(1024)S(1)}, u32[]{:S(2)}) copy-start(f32[2048]{0:T(1024)S(1)} %get-tuple-element.27) | copy-start | bytes 24580
  99.3 19.7 %copy-start.5 = (bf16[2048,640]{0,1:T(8,128)(2,1)S(1)}, bf16[2048,640]{0,1:T(8,128)(2,1)}, u32[]{:S(2)}) copy-start(bf16[2048,640]{0,1:T(8,128)(2,1)} %get-tuple-element.28) | copy-start | bytes 7864324
  211.0 17.4 %copy-start.9 = (f32[2048]{0:T(1024)S(1)}, f32[2048]{0:T(1024)}, u32[]{:S(2)}) copy-start(f32[2048]{0:T(1024)} %copy-done.8) | copy-start | bytes 24580
  235.7 1.5 copy-start.7
  288.9 17.9 %slice-start = ((s8[16777216]{0:T(1024)(128)(4,1)}), s8[4194304]{0:T(1024)(128)(4,1)S(1)}, s32[]{:S(2)}) async-start(s8[16777216]{0:T(1024)(128)(4,1)} %bitcast.143), calls=%async_computation | async-start | bytes 8388608
  288.9 17.9 %slice-start.1 = ((s8[16777216]{0:T(1024)(128)(4,1)}), s8[4194304]{0:T(1024)(128)(4,1)S(1)}, s32[]{:S(2)}) async-start(s8[16777216]{0:T(1024)(128)(4,1)} %bitcast.143), calls=%async_computation.1 | async-start | bytes 8388608
  288.9 17.9 %slice-start.2 = ((s8[16777216]{0:T(1024)(128)(4,1)}), s8[4194304]{0:T(1024)(128)(4,1)S(1)}, s32[]{:S(2)}) async-start(s8[16777216]{0:T(1024)(128)(4,1)} %bitcast.143), calls=%async_computation.2 | async-start | bytes 8388608
  300.1 6.7 copy-start.6
  300.1 6.6 slice-start.3
  319.7 19.7 %copy-start.3 = (bf16[1,2048,640]{1,2,0:T(8,128)(2,1)S(1)}, bf16[1,2048,640]{1,2,0:T(8,128)(2,1)}, u32[]{:S(2)}) copy-start(bf16[1,2048,640]{1,2,0:T(8,128)(2,1)} %copy-done.2) | copy-start | bytes 7864324
  319.7 19.7 %copy-start.11 = (f32[2048]{0:T(1024)S(1)}, f32[2048]{0:T(1024)}, u32[]{:S(2)}) copy-start(f32[2048]{0:T(1024)} %copy-done.10) | copy-start | bytes 24580
  961.9 8.1 copy-start
  1147.6 17.8 %copy-start.4 = (bf16[2,4,1,4,1,160,128]{6,5,3,1,0,4,2:T(8,128)(2,1)S(1)}, bf16[2,4,1,4,1,160,128]{6,5,3,1,0,4,2:T(8,128)(2,1)}, u32[]{:S(2)}) copy-start(bf16[2,4,1,4,1,160,128]{6,5,3,1,0,4,2:T(8,128)(2,1)} %get-tuple-element.16) | copy-start | bytes 3932164
  1165.9 8.9 copy-start.1

commit v2 on v0

v2 whole, which is shorter than its diff:
```python
import jax
import jax.numpy as jnp
from jax import lax
from jax.experimental import pallas as pl
from jax.experimental.pallas import tpu as pltpu
from jax.sharding import PartitionSpec as P

MESH = pl.DeviceIdType.MESH
BF, F32 = jnp.bfloat16, jnp.float32

T, D, FF = 2048, 640, 4096
DEVICES, CHIPS, LANE = 8, 4, 128
TILE = DEVICES * LANE
ROWS, TALL = D // DEVICES, FF // DEVICES
PIECE, BLOCK = 512, 256

ROUNDS, MR, SUB = 96, 160, 32
PER_TILE = 12
D0, LAG, LAGF, LAGA, LAGD = 2, 2, 2, 2, 2
RING, SLOTS, KEPT = 16, 4, 12
TICKS = ROUNDS + D0 + 3 * LAG + LAGF + 2 * LAGA + max(LAGD, SLOTS)
AHEAD = 8


def normed(h):
    wide = h.astype(F32)
    scale = lax.rsqrt(jnp.mean(wide**2, -1, keepdims=True) + 1e-6)
    return (wide * scale).astype(BF)


def dot(a, b):
    return jnp.dot(a, b, preferred_element_type=F32)


def across(a, b):
    return lax.dot_general(a, b, (((1,), (1,)), ((), ())), preferred_element_type=F32)


def moments(m, v, g):
    return 0.9 * m + 0.1 * g, 0.95 * v + 0.05 * g * g


def within(r):
    return (r >= 0) & (r < ROUNDS)


def most(zp):
    return jnp.maximum(zp, CHIPS - 1 - zp)


def part(i, n):
    return pl.ds(pl.multiple_of(n * i, n), n)


def cut(i, n):
    return slice(n * i, n * i + n)


def times(n, first=0):
    return pl.loop(first, n)


def kernel(
    x, dy, w_g, w_u, w_d, m_g, m_u, m_d, v_g, v_u, v_d,
    news, grads, terms,
    mine, others, line, summed, fresh, final, wb, mb, vb, wdb, mdb, vdb,
    hv, xv, av, at, ct, ctt, wgt, wut, wdt, act, dgate, dup, dag, dau, staged, staged_d,
    sem_pair_s, sem_pair_r, sem_line_s, sem_line_r, sem_mine, sem_state, sem_own, sem_ag_s, sem_ag_r, sem_agp_s, sem_agp_r, sem_own_r,
    sem_in, sem_w, sem_st,
):
    def tile(t):
        slot, of, j = lax.rem(t, 2), lax.rem(lax.div(t, CHIPS), 2), lax.rem(t, CHIPS)
        sems = [sem_w.at[i, slot] for i in range(3)]
        for d in range(DEVICES):
            cols, to = pl.ds(pl.multiple_of(TALL * d + LANE * j, LANE), LANE), pl.ds(LANE * d, LANE)
            pltpu.make_async_copy(w_g.at[of, :, cols], wgt.at[slot, :, to], sems[0]).start()
            pltpu.make_async_copy(w_u.at[of, :, cols], wut.at[slot, :, to], sems[1]).start()
            pltpu.make_async_copy(w_d.at[of, cols], wdt.at[slot, to], sems[2]).start()

    def tile_wait(t):
        slot, all_of = lax.rem(t, 2), pl.ds(0, TILE)
        sems = [sem_w.at[i, slot] for i in range(3)]
        pltpu.make_async_copy(w_g.at[0, :, all_of], wgt.at[slot], sems[0]).wait()
        pltpu.make_async_copy(w_u.at[0, :, all_of], wut.at[slot], sems[1]).wait()
        pltpu.make_async_copy(w_d.at[0, all_of], wdt.at[slot], sems[2]).wait()

    line[...] = jnp.zeros_like(line)
    load_x, load_dy = pltpu.make_async_copy(x, xv, sem_in.at[0]), pltpu.make_async_copy(dy, ct, sem_in.at[1])
    load_x.start()
    tile(0)
    load_dy.start()
    tile(1)

    me = lax.axis_index("dp")
    z, c = lax.div(me, 2), lax.rem(me, 2)
    partner = me + 1 - 2 * c
    low, high = z > 0, z < CHIPS - 1

    barrier = pltpu.get_barrier_semaphore()

    def greet(dev):
        pl.semaphore_signal(barrier, inc=1, device_id={"dp": dev}, device_id_type=MESH)

    greet(partner)
    pl.when(low)(lambda: greet(me - 2))
    pl.when(high)(lambda: greet(me + 2))

    def remote(src, dst, send, recv, dev):
        return pltpu.make_async_remote_copy(src, dst, send, recv, device_id={"dp": dev}, device_id_type=MESH)

    def pair(r):
        slot, kept = lax.rem(r, SLOTS), lax.rem(r, KEPT)
        return remote(terms.at[r, 1 - c], others.at[kept], sem_pair_s.at[slot], sem_pair_r.at[kept], partner)

    def own_terms(r):
        kept = lax.rem(r, KEPT)
        return pltpu.make_async_copy(terms.at[r, c], mine.at[kept], sem_mine.at[kept])

    def arrival(r, place):
        ring = lax.rem(r, RING)
        return remote(summed.at[0, 0], line.at[place, ring], sem_line_s.at[0, 0], sem_line_r.at[place, ring], partner)

    def on_chip(r, zp):
        kept = lax.rem(r, KEPT)
        return mine[kept, zp].astype(F32) + others[kept, zp].astype(F32)

    class Line:
        def __init__(self, i, k):
            self.i, self.zp = i, lax.rem(z + 1 + i, CHIPS)
            self.right = self.zp > z
            self.r = k - D0 - LAG * jnp.where(self.right, z, CHIPS - 1 - z)
            self.ok = within(self.r)
            self.fed = self.ok & jnp.where(self.right, low, high)

        def send(self, r):
            nxt = jnp.where(self.right, z + 1, z - 1)
            place = jnp.where((nxt == self.zp) & ~self.right, CHIPS, self.zp)
            slot, ring = lax.rem(r, SLOTS), lax.rem(r, RING)
            return remote(summed.at[self.i, slot], line.at[place, ring], sem_line_s.at[self.i, slot], sem_line_r.at[place, ring], 2 * nxt + c)

        def step(self):
            pl.when(within(self.r - SLOTS))(lambda: self.send(self.r - SLOTS).wait_send())
            pl.when(self.fed)(lambda: arrival(self.r, self.zp).wait_recv())

            @pl.when(self.ok)
            def _():
                total = on_chip(self.r, self.zp) + line[self.zp, lax.rem(self.r, RING)].astype(F32)
                summed[self.i, lax.rem(self.r, SLOTS)] = total.astype(BF)
                self.send(self.r).start()

    def state(r, go):
        in_tile = lax.rem(r, PER_TILE)
        kind, q, t = lax.div(in_tile, CHIPS), lax.rem(r, CHIPS), lax.div(r, PER_TILE)
        of, j = 1 - lax.div(t, CHIPS), lax.rem(t, CHIPS)
        for number, (w, m, v) in enumerate(((w_g, m_g, v_g), (w_u, m_u, v_u))):

            @pl.when(kind == number)
            def _(w=w, m=m, v=v):
                rows = pl.ds(pl.multiple_of(ROWS * me, 16), ROWS)
                for s in range(2):
                    cols = pl.ds(pl.multiple_of(TALL * (2 * q + s) + LANE * j, LANE), LANE)
                    to, sems = pl.ds(ROWS * s, ROWS), [sem_state.at[i, s] for i in range(3)]
                    go(pltpu.make_async_copy(w.at[of, rows, cols], wb.at[to], sems[0]))
                    go(pltpu.make_async_copy(m.at[of, :, cols], mb.at[to], sems[1]))
                    go(pltpu.make_async_copy(v.at[of, :, cols], vb.at[to], sems[2]))

        @pl.when(kind == 2)
        def _():
            row, sems = pl.multiple_of(LANE * j + SUB * q, SUB), [sem_state.at[i, 0] for i in range(3)]
            rows = pl.ds(row, SUB)
            go(pltpu.make_async_copy(w_d.at[of, pl.ds(pl.multiple_of(TALL * me + row, SUB), SUB)], wdb, sems[0]))
            go(pltpu.make_async_copy(m_d.at[of, rows], mdb, sems[1]))
            go(pltpu.make_async_copy(v_d.at[of, rows], vdb, sems[2]))

    def adamw(w, m, v, g):
        m, v = moments(m, v, g.astype(F32))
        w = w.astype(F32)
        return (w - 0.02 * (m * lax.rsqrt(v + 1e-8) + 0.1 * w)).astype(BF)

    class Own:
        def __init__(self, k):
            self.r = k - D0 - LAG * most(z)
            self.ok = within(self.r)

        def outs(self, r, go):
            slot, ring = lax.rem(r, SLOTS), lax.rem(r, RING)
            src, dst = fresh.at[slot], news.at[r, c, z]
            pl.when(high)(lambda: go(remote(src, dst, sem_own.at[0, slot], sem_ag_r.at[z, ring], me + 2)))
            pl.when(low)(lambda: go(remote(src, dst, sem_own.at[1, slot], sem_ag_r.at[z, ring], me - 2)))
            go(remote(src, dst, sem_own.at[2, slot], sem_own_r.at[ring], partner))

        def local(self, r, go):
            slot = lax.rem(r, SLOTS)
            go(pltpu.make_async_copy(fresh.at[slot], news.at[r, c, z], sem_own.at[3, slot]))
            go(pltpu.make_async_copy(final.at[slot], grads.at[r], sem_own.at[4, slot]))

        def step(self):
            @pl.when(within(self.r - SLOTS))
            def _():
                self.outs(self.r - SLOTS, lambda d: d.wait_send())
                self.local(self.r - SLOTS, lambda d: d.wait())

            pl.when(self.ok & low)(lambda: arrival(self.r, z).wait_recv())
            pl.when(self.ok & high)(lambda: arrival(self.r, CHIPS).wait_recv())

            @pl.when(self.ok)
            def _():
                slot, ring = lax.rem(self.r, SLOTS), lax.rem(self.r, RING)
                tall = lax.rem(self.r, PER_TILE) >= 2 * CHIPS
                total = on_chip(self.r, z) + line[z, ring].astype(F32) + line[CHIPS, ring].astype(F32)
                final[slot] = total.astype(BF)
                state(self.r, lambda d: d.wait())

                @pl.when(tall)
                def _():
                    for i in range(D // LANE):
                        rows, cols = pl.ds(SUB * i, SUB), pl.ds(LANE * i, LANE)
                        fresh[slot, rows] = adamw(wdb[:, cols], mdb[:, cols], vdb[:, cols], final[slot, rows])

                @pl.when(jnp.logical_not(tall))
                def _():
                    fresh[slot] = adamw(wb[...], mb[...], vb[...], final[slot])

                self.outs(self.r, lambda d: d.start())
                self.local(self.r, lambda d: d.start())

            pl.when(within(self.r + 1))(lambda: state(self.r + 1, lambda d: d.start()))

    def sent(k, zp):
        away = jnp.abs(z - zp)
        return k - D0 - LAG * most(zp) - LAGA * away - (LAGF - LAGA) * jnp.minimum(away, 1)

    class Gather:
        def __init__(self, i, k):
            self.i, self.zp = i, lax.rem(z + 1 + i, CHIPS)
            self.r, self.up = sent(k, self.zp), self.zp < z
            self.on = jnp.where(self.up, high, low)

        def forward(self, r):
            nxt, spot = jnp.where(self.up, z + 1, z - 1), news.at[r, c, self.zp]
            return remote(spot, spot, sem_ag_s.at[self.i, lax.rem(r, SLOTS)], sem_ag_r.at[self.zp, lax.rem(r, RING)], 2 * nxt + c)

        def over(self, r):
            return bundle(r, c, self.zp, sem_agp_s.at[self.i, lax.rem(lax.div(r, SLOTS), 2)])

        def step(self):
            old, now, last = within(self.r - SLOTS), within(self.r), lax.rem(self.r, SLOTS) == SLOTS - 1
            pl.when(old & self.on)(lambda: self.forward(self.r - SLOTS).wait_send())
            pl.when(old & last)(lambda: self.over(self.r - SLOTS).wait_send())
            pl.when(now)(lambda: self.forward(self.r).wait_recv())
            pl.when(now & self.on)(lambda: self.forward(self.r).start())
            pl.when(now & last)(lambda: self.over(self.r).start())

    def bundle(r, core, zp, send):
        spot = news.at[pl.ds(r - (SLOTS - 1), SLOTS), core, zp]
        return remote(spot, spot, send, sem_agp_r.at[zp, lax.rem(lax.div(r, SLOTS), SLOTS)], partner)

    def tick(k):
        pl.when(within(k - SLOTS))(lambda: pair(k - SLOTS).wait_send())

        @pl.when(within(k))
        def _():
            pair(k).start()
            own_terms(k).start()

        @pl.when(within(k - D0))
        def _():
            pair(k - D0).wait_recv()
            own_terms(k - D0).wait()

        for i in range(CHIPS - 1):
            Line(i, k).step()
        for i in range(CHIPS - 1):
            Gather(i, k).step()
        Own(k).step()
        r = sent(k, z) - LAGD
        spot = news.at[r, 1 - c, z]
        pl.when(within(r))(lambda: remote(spot, spot, sem_agp_s.at[0, 0], sem_own_r.at[lax.rem(r, RING)], partner).wait_recv())
        for i in range(CHIPS - 1):
            zp = lax.rem(z + 1 + i, CHIPS)
            r = sent(k, zp) - LAGD
            done = within(r) & (lax.rem(r, SLOTS) == SLOTS - 1)
            pl.when(done)(lambda r=r, zp=zp: bundle(r, 1 - c, zp, sem_agp_s.at[0, 0]).wait_recv())

    load_x.wait()
    half = T // 2

    @times(T // BLOCK)
    def _(p):
        rows = part(p, BLOCK)
        av[rows] = normed(xv[rows])
        dag[rows] = jnp.zeros((BLOCK, D), F32)

    def hidden(i):
        slot, rows = lax.rem(lax.div(i, 2), 2), part(lax.rem(i, 2), half)
        a = av[rows]
        for n in range(TILE // PIECE):
            cols = pl.ds(PIECE * n, PIECE)
            gate, up = dot(a, wgt[slot, :, cols]), dot(a, wut[slot, :, cols])
            act[rows, cols] = (gate * jax.nn.sigmoid(gate) * up).astype(BF)

    def turn(i):
        rows = part(i, BLOCK)
        ctt[:, rows] = ct[rows].T

    def back(i):
        slot, rows = lax.rem(lax.div(i, 2), 2), part(lax.rem(i, 2), half)
        dag[rows] = dag[rows] + dot(act[rows], wdt[slot])

    tile_wait(0)
    hidden(0)
    load_dy.wait()
    turn(0)

    @times(2 * CHIPS, first=1)
    def _(i):
        first, t = lax.rem(i, 2) == 0, lax.div(i, 2)
        pl.when(first)(lambda: tile_wait(t))
        pl.when(jnp.logical_not(first) & (t > 0))(lambda: tile(t + 1))
        back(i - 1)
        hidden(i)
        turn(i)

    back(2 * CHIPS - 1)

    @times(T // BLOCK)
    def _(p):
        rows = part(p, BLOCK)
        h = xv[rows] + dag[rows].astype(BF)
        a = normed(h)
        hv[rows], av[rows], at[:, rows] = h, a, a.T
        dag[rows] = dau[rows] = jnp.zeros((BLOCK, D), F32)

    def next_layer(q):
        @times(PIECE // BLOCK)
        def _(i):
            rows = part(PIECE // BLOCK * q + i, BLOCK)
            da = (dag[rows].astype(BF) + dau[rows].astype(BF)).astype(F32)
            wide = hv[rows].astype(F32)
            mean = jnp.mean(wide * wide, -1, keepdims=True) + 1e-6
            scale = lax.rsqrt(mean)
            along = jnp.sum(da * wide, -1, keepdims=True) * (-scale / (D * mean))
            by = ct[rows] + (da * scale + wide * along).astype(BF)
            a = normed(xv[rows])
            ct[rows], ctt[:, rows], av[rows], at[:, rows] = by, by.T, a, a.T

    def tokens(slot, p):
        rows = part(p, PIECE)
        a, by = av[rows], ct[rows]
        for n in range(TILE // PIECE):
            cols = pl.ds(PIECE * n, PIECE)
            gate, up = dot(a, wgt[slot, :, cols]), dot(a, wut[slot, :, cols])
            dact = across(by, wdt[slot, cols]).astype(BF).astype(F32)
            sig = jax.nn.sigmoid(gate)
            silu = gate * sig
            act[rows, cols] = (silu * up).astype(BF)
            dup[rows, cols] = (dact * silu).astype(BF)
            dgate[rows, cols] = (dact * up * (sig + silu * (1.0 - sig))).astype(BF)

    def put(slot, r):
        return pltpu.make_async_copy(staged.at[slot], terms.at[r], sem_st.at[slot])

    def put_d(t, go):
        for q in range(CHIPS):
            go(pltpu.make_async_copy(staged_d.at[q], terms.at[PER_TILE * t + 2 * CHIPS + q], sem_st.at[2 + q]))

    def wide_terms(by, slot, q, r):
        g = dot(at[...], by[:, part(q, BLOCK)]).astype(BF)
        for d in range(DEVICES):
            for s in range(2):
                staged[slot, d % 2, d // 2, cut(s, ROWS)] = g[cut(d, ROWS), cut(s, LANE)]
        put(slot, r).start()

    def down_terms(i):
        g = dot(ctt[...], act[:, part(i, BLOCK)]).T.astype(BF)
        for o in range(2):
            for q in range(CHIPS):
                for s in range(D // LANE):
                    staged_d[q, o, i, cut(s, SUB)] = g[cut(CHIPS * o + q, SUB), cut(s, LANE)]

    def by_normed(to, by, w, slot, p):
        rows = part(p, PIECE)
        to[rows] = to[rows] + across(by[rows], w[slot])

    pl.semaphore_wait(barrier, 1 + low.astype(jnp.int32) + high.astype(jnp.int32))

    @times(TICKS + AHEAD)
    def _(n):
        q, phase, t = lax.rem(n, CHIPS), lax.div(lax.rem(n, PER_TILE), CHIPS), lax.div(n, PER_TILE)
        slot, busy = lax.rem(t, 2), n < ROUNDS

        @pl.when(busy & (phase == 0) & (q == 0))
        def _():
            tile_wait(t)
            pl.when(n < ROUNDS - PER_TILE)(lambda: tile(t + CHIPS + 1))

        pl.when((n > 0) & (n <= ROUNDS) & (lax.rem(n - 1, PER_TILE) >= CHIPS))(lambda: put(lax.rem(n - 1, 2), n - 1 - CHIPS).wait())
        pl.when((phase == 0) & (q == 2) & (n >= PER_TILE) & (n < ROUNDS + PER_TILE))(lambda: put_d(t - 1, lambda d: d.wait()))

        def work():
            @pl.when(busy & (phase == 0))
            def _():
                pl.when(t == CHIPS)(lambda: next_layer(q))
                tokens(slot, q)

            @pl.when(busy & (phase == 1))
            def _():
                wide_terms(dgate, lax.rem(n, 2), q, n - CHIPS)
                pl.when((t > 0) & (t < CHIPS))(lambda: by_normed(dag, dgate, wgt, slot, q))

            @pl.when(busy & (phase == 2))
            def _():
                wide_terms(dup, lax.rem(n, 2), q, n - CHIPS)
                down_terms(q)
                pl.when(t == 0)(lambda: by_normed(dag, dgate, wgt, slot, q))
                pl.when(t < CHIPS)(lambda: by_normed(dau, dup, wut, slot, q))
                pl.when(q == CHIPS - 1)(lambda: put_d(t, lambda d: d.start()))

        tick(n - AHEAD)
        work()


def backward(x, dy, weights, m, v):
    def dma(*shape):
        return pltpu.SemaphoreType.DMA(shape)

    def bf(*shape):
        return pltpu.VMEM(shape, BF)

    def f32(*shape):
        return pltpu.VMEM(shape, F32)

    message = (MR, LANE)
    outs = ((2, CHIPS, *message), message, (2, CHIPS, *message))
    anywhere = pl.BlockSpec(memory_space=pl.ANY)
    return pl.pallas_call(
        kernel,
        name="backward",
        out_shape=[jax.ShapeDtypeStruct((ROUNDS, *s), BF) for s in outs],
        in_specs=[anywhere] * 11,
        out_specs=[anywhere] * len(outs),
        scratch_shapes=[
            bf(KEPT, CHIPS, *message), bf(KEPT, CHIPS, *message), bf(CHIPS + 1, RING, *message), bf(3, SLOTS, *message), bf(SLOTS, *message), bf(SLOTS, *message),
            bf(*message), f32(*message), f32(*message), bf(SUB, D), f32(SUB, D), f32(SUB, D),
            bf(T, D), bf(T, D), bf(T, D), bf(D, T), bf(T, D), bf(D, T),
            bf(2, D, TILE), bf(2, D, TILE), bf(2, TILE, D),
            bf(T, TILE), bf(T, TILE), bf(T, TILE), f32(T, D), f32(T, D),
            bf(2, 2, CHIPS, *message), bf(CHIPS, 2, CHIPS, *message),
            dma(SLOTS), dma(KEPT), dma(3, SLOTS), dma(CHIPS + 1, RING), dma(KEPT), dma(3, 2), dma(5, SLOTS),
            dma(3, SLOTS), dma(CHIPS, RING), dma(3, 2), dma(CHIPS, SLOTS), dma(RING),
            dma(2), dma(3, 2), dma(2 + CHIPS),
        ],
        compiler_params=pltpu.CompilerParams(collective_id=0, has_side_effects=True, vmem_limit_bytes=67_043_328),
    )(x, dy, *weights, *m, *v)


DEPTH, STORES = 4, 3


def finish_kernel(*refs):
    def three(first):
        return refs[first : first + 3]

    news, grads, m, v = refs[0], refs[1], three(2), three(5)
    w_out, m_out, v_out = three(8), three(11), three(14)
    new_in, grad_in, m_in, v_in = three(17), three(20), three(23), three(26)
    w_to, m_to, v_to = three(29), three(32), three(35)
    sem_in, sem_out = refs[38:]
    steps = 2 * DEVICES

    def where(i):
        n, d = lax.div(i, DEVICES), lax.rem(i, DEVICES)
        wide, tall = pl.ds(pl.multiple_of(PIECE * d, PIECE), PIECE), pl.ds(pl.multiple_of(2 * SUB * d, 2 * SUB), 2 * SUB)
        return n, d, [(n, slice(None), wide)] * 2 + [(n, tall)]

    def loads(i, go):
        slot = lax.rem(i, DEPTH)
        n, d, states = where(i)
        core, chip, of = lax.rem(d, 2), lax.div(d, 2), 1 - n
        for kind in range(3):
            if kind < 2:
                grad = grads.at[of, :, kind, chip]
            else:
                grad = grads.at[of, chip, kind, pl.ds(2 * core, 2)]
            pairs = (
                (news.at[of, :, kind, :, core, chip], new_in[kind]),
                (grad, grad_in[kind]),
                (m[kind].at[states[kind]], m_in[kind]),
                (v[kind].at[states[kind]], v_in[kind]),
            )
            for number, (src, dst) in enumerate(pairs):
                go(pltpu.make_async_copy(src, dst.at[slot], sem_in.at[slot, kind, number]))

    def stores(i, go):
        slot = lax.rem(i, STORES)
        n, d, states = where(i)
        rows, tall = pl.ds(pl.multiple_of(ROWS * d, 16), ROWS), pl.ds(pl.multiple_of(TALL * d, TALL), TALL)
        for kind in range(3):
            pairs = (
                (w_to[kind], w_out[kind].at[n, rows if kind < 2 else tall]),
                (m_to[kind], m_out[kind].at[states[kind]]),
                (v_to[kind], v_out[kind].at[states[kind]]),
            )
            for number, (src, dst) in enumerate(pairs):
                go(pltpu.make_async_copy(src.at[slot], dst, sem_out.at[slot, kind, number]))

    for first in range(DEPTH):
        loads(first, lambda d: d.start())

    @times(steps)
    def _(i):
        slot, to, s = lax.rem(i, DEPTH), lax.rem(i, STORES), lax.rem(i, 2)
        loads(i, lambda d: d.wait())
        pl.when(i >= STORES)(lambda: stores(i - STORES, lambda d: d.wait()))

        def step(kind, rows, cols, g):
            old_m, old_v = m_in[kind][slot, rows, cols], v_in[kind][slot, rows, cols]
            m_to[kind][to, rows, cols], v_to[kind][to, rows, cols] = moments(old_m, old_v, g.astype(F32))

        for kind in range(2):
            for j in range(CHIPS):
                for q in range(CHIPS):
                    for half in range(2):
                        w_to[kind][to, :, cut(4 * (2 * q + half) + j, LANE)] = new_in[kind][slot, j, q, cut(half, ROWS)]
                step(kind, slice(ROWS), cut(j, LANE), grad_in[kind][slot, j, part(s, ROWS)])
        for number in range(D // LANE):
            for j in range(CHIPS):
                for q in range(CHIPS):
                    w_to[2][to, cut(CHIPS * j + q, SUB), cut(number, LANE)] = new_in[2][slot, j, q, cut(number, SUB)]
            for q in range(2):
                step(2, cut(q, SUB), cut(number, LANE), grad_in[2][slot, q, cut(number, SUB)])
        stores(i, lambda d: d.start())
        pl.when(i < steps - DEPTH)(lambda: loads(i + DEPTH, lambda d: d.start()))

    for last in range(STORES):
        stores(steps - STORES + last, lambda d: d.wait())


def finish(news, grads, m, v):
    shape = (2, CHIPS, 3, CHIPS)
    news, grads = news.reshape(*shape, 2, CHIPS, MR, LANE), grads.reshape(*shape, MR, LANE)
    anywhere = pl.BlockSpec(memory_space=pl.ANY)
    blocks = [(ROWS, PIECE), (ROWS, PIECE), (2 * SUB, D)]
    states = [jax.ShapeDtypeStruct(a.shape, F32) for a in m]
    return pl.pallas_call(
        finish_kernel,
        name="finish",
        out_shape=[*[jax.ShapeDtypeStruct((2, D, FF), BF)] * 2, jax.ShapeDtypeStruct((2, FF, D), BF), *states * 2],
        in_specs=[anywhere] * 8,
        out_specs=[anywhere] * 9,
        scratch_shapes=[
            *[pltpu.VMEM((DEPTH, CHIPS, CHIPS, MR, LANE), BF)] * 3,
            *[pltpu.VMEM((DEPTH, n, MR, LANE), BF) for n in (CHIPS, CHIPS, 2)],
            *[pltpu.VMEM((DEPTH, *b), F32) for b in blocks * 2],
            *[pltpu.VMEM((STORES, *b), BF) for b in ((ROWS, FF), (ROWS, FF), (TALL, D))],
            *[pltpu.VMEM((STORES, *b), F32) for b in blocks * 2],
            pltpu.SemaphoreType.DMA((DEPTH, 3, 4)), pltpu.SemaphoreType.DMA((STORES, 3, 3)),
        ],
        compiler_params=pltpu.CompilerParams(vmem_limit_bytes=60 * 2**20),
    )(news, grads, *m, *v)


def solution(mesh):
    def step(x, dy, *arrays):
        weights, m, v = (arrays[i : i + 3] for i in (0, 3, 6))
        news, grads, *_ = backward(x[0], dy[0], weights, m, v)
        return tuple(finish(news, grads, m, v))

    by_device, whole, rows = P(("rep", "dp")), P(), P(None, "dp")
    return jax.shard_map(
        step,
        mesh=mesh,
        in_specs=(by_device,) * 2 + (whole,) * 3 + (rows,) * 6,
        out_specs=(P("rep"),) * 3 + (P("rep", "dp"),) * 6,
        check_vma=False,
    )
```

time: 1270 us -> 488 us (0.38)
  waiting for transfers between devices: 778 us -> 0 us
  Pallas kernels: 0 us -> 487 us
  matrix products: 326 us -> 0 us
  other arithmetic: 93.9 us -> 0 us
  local copies, waits for them, and re-layouts: 45.8 us -> 0 us
  between operations: 15.2 us -> 0.81 us
    pallas_call x0 -> x2, Pallas kernels: none -> 487 us  [the longest x1 454 us: backward(): pl.pallas_call(kernel, name='backward', out_shape=[jax.ShapeDtypeStruct((...]
    unnamed x15 -> x0, waiting for transfers between devices: 486 us -> none
    dot_general x15 -> x0, matrix products: 326 us -> none  [the longest x5 115 us: layer(): up = jnp.dot(a, w['w_up'], preferred_element_type=jnp.float32)]
    reshape x3 -> x0, waiting for transfers between devices: 291 us -> none  [step(): t.reshape(-1, *t.shape[2:])]
    unnamed x3 -> x0, other arithmetic: 64.2 us -> none
    unnamed x43 -> x0, local copies, waits for them, and re-layouts: 45.2 us -> none
    reshape x3 -> x0, other arithmetic: 18.9 us -> none  [step(): t.reshape(-1, *t.shape[2:])]
  transfers between devices with their start and end apart: 9 -> 0, of which waited for: 8 -> 0; matrix products, arithmetic and copies ran while one was open for 14% -> 0% of each run, Pallas kernels for 0% -> 0%
where the time goes in v2:
time: 488 us
  Pallas kernels  487 us (100%)
    pallas_call x1, Pallas kernels, backward(): pl.pallas_call(kernel, name='backward', out_shape=[jax.ShapeDtypeStruct((...  454 us
    pallas_call x1, Pallas kernels, finish(): pl.pallas_call(finish_kernel, name='finish', out_shape=[*[jax.ShapeDtypeS...  33.6 us

profile of v2, /device:TPU:0, one launch (start us, length us, event | category | flops | bytes accessed | tf_op | source)
XLA Modules:
  0.0 488.0 jit_solution(13563177573840013878)
XLA Ops:
  0.6 453.7 %backward.1 = (bf16[96,2,4,160,128]{4,3,2,1,0:T(8,128)(2,1)}, bf16[96,160,128]{2,1,0:T(8,128)(2,1)}, bf16[96,2,4,160,128]{4,3,2,1,0:T(8,128)(2,1)}) custom-call(bf16[2048,640]{1,0:T(8,128)(2,1)} %bitcast.6, bf16[2048,640]{1,0:T(8,128)(2,1)} %bitcast.7, bf16[2,640,4096]{2,1,0:T(8,128)(2,1)} %w_g.1, bf16[2,640,4096]{2,1,0:T(8,128)(2,1)} %w_u.1, ...), custom_call_target="tpu_custom_call" | custom-call | tf_op jit(solution)/shard_map/backward/pallas_call | solution.py:436
  454.3 33.6 %finish.1 = (bf16[2,640,4096]{2,1,0:T(8,128)(2,1)}, bf16[2,640,4096]{2,1,0:T(8,128)(2,1)}, bf16[2,4096,640]{2,1,0:T(8,128)(2,1)}, f32[2,80,4096]{2,1,0:T(8,128)}...) custom-call(bf16[2,4,3,4,2,4,160,128]{7,6,5,4,3,2,1,0:T(8,128)(2,1)}, ...), custom_call_target="tpu_custom_call" | custom-call | tf_op jit(solution)/shard_map/finish/pallas_call | solution.py:545

commit v3 on v2

--- a/solution.py
+++ b/solution.py
@@ -16,10 +16,10 @@
 
 ROUNDS, MR, SUB = 96, 160, 32
 PER_TILE = 12
-D0, LAG, LAGF, LAGA, LAGD = 2, 2, 2, 2, 2
+D0, LAG, LAGF, LAGA, LAGD = 2, 2, 3, 3, 2
 RING, SLOTS, KEPT = 16, 4, 12
 TICKS = ROUNDS + D0 + 3 * LAG + LAGF + 2 * LAGA + max(LAGD, SLOTS)
-AHEAD = 8
+AHEAD = 6
 
 
 def normed(h):
@@ -42,6 +42,25 @@
 
 def within(r):
     return (r >= 0) & (r < ROUNDS)
+
+
+def stage(n):
+    t = lax.div(n, PER_TILE)
+    return t, lax.rem(n, PER_TILE), lax.rem(t, CHIPS) == 0
+
+
+def plan(r):
+    t, i, early = stage(r + CHIPS)
+    late = i - CHIPS
+    kind = jnp.where(early, jnp.where(late < 0, 2, lax.rem(late, 2)), lax.rem(i, 3))
+    q = jnp.where(early, jnp.where(late < 0, i, lax.div(late, 2)), lax.div(i, 3))
+    t = t - lax.div(kind, 2)
+    return PER_TILE * t + CHIPS * kind + q, t, kind, q
+
+
+def ends_kind(r):
+    _, i, early = stage(r + CHIPS)
+    return jnp.where(early, (i == 3) | (i >= PER_TILE - 2), i >= PER_TILE - 3)
 
 
 def most(zp):
@@ -85,9 +104,12 @@
         pltpu.make_async_copy(w_d.at[0, all_of], wdt.at[slot], sems[2]).wait()
 
     line[...] = jnp.zeros_like(line)
-    load_x, load_dy = pltpu.make_async_copy(x, xv, sem_in.at[0]), pltpu.make_async_copy(dy, ct, sem_in.at[1])
+    upper, lower = pl.ds(0, T // 2), pl.ds(T // 2, T // 2)
+    load_x, load_more = (pltpu.make_async_copy(x.at[rows], xv.at[rows], sem_in.at[i]) for i, rows in enumerate((upper, lower)))
+    load_dy = pltpu.make_async_copy(dy, ct, sem_in.at[2])
     load_x.start()
     tile(0)
+    load_more.start()
     load_dy.start()
     tile(1)
 
@@ -108,13 +130,13 @@
     def remote(src, dst, send, recv, dev):
         return pltpu.make_async_remote_copy(src, dst, send, recv, device_id={"dp": dev}, device_id_type=MESH)
 
-    def pair(r):
+    def pair(r, at_round=0):
         slot, kept = lax.rem(r, SLOTS), lax.rem(r, KEPT)
-        return remote(terms.at[r, 1 - c], others.at[kept], sem_pair_s.at[slot], sem_pair_r.at[kept], partner)
-
-    def own_terms(r):
+        return remote(terms.at[at_round, 1 - c], others.at[kept], sem_pair_s.at[slot], sem_pair_r.at[kept], partner)
+
+    def own_terms(r, at_round=0):
         kept = lax.rem(r, KEPT)
-        return pltpu.make_async_copy(terms.at[r, c], mine.at[kept], sem_mine.at[kept])
+        return pltpu.make_async_copy(terms.at[at_round, c], mine.at[kept], sem_mine.at[kept])
 
     def arrival(r, place):
         ring = lax.rem(r, RING)
@@ -149,8 +171,7 @@
                 self.send(self.r).start()
 
     def state(r, go):
-        in_tile = lax.rem(r, PER_TILE)
-        kind, q, t = lax.div(in_tile, CHIPS), lax.rem(r, CHIPS), lax.div(r, PER_TILE)
+        _, t, kind, q = plan(r)
         of, j = 1 - lax.div(t, CHIPS), lax.rem(t, CHIPS)
         for number, (w, m, v) in enumerate(((w_g, m_g, v_g), (w_u, m_u, v_u))):
 
@@ -182,17 +203,17 @@
             self.r = k - D0 - LAG * most(z)
             self.ok = within(self.r)
 
-        def outs(self, r, go):
+        def outs(self, r, go, at_round=0):
             slot, ring = lax.rem(r, SLOTS), lax.rem(r, RING)
-            src, dst = fresh.at[slot], news.at[r, c, z]
+            src, dst = fresh.at[slot], news.at[at_round, c, z]
             pl.when(high)(lambda: go(remote(src, dst, sem_own.at[0, slot], sem_ag_r.at[z, ring], me + 2)))
             pl.when(low)(lambda: go(remote(src, dst, sem_own.at[1, slot], sem_ag_r.at[z, ring], me - 2)))
             go(remote(src, dst, sem_own.at[2, slot], sem_own_r.at[ring], partner))
 
-        def local(self, r, go):
+        def local(self, r, go, at_round=0):
             slot = lax.rem(r, SLOTS)
-            go(pltpu.make_async_copy(fresh.at[slot], news.at[r, c, z], sem_own.at[3, slot]))
-            go(pltpu.make_async_copy(final.at[slot], grads.at[r], sem_own.at[4, slot]))
+            go(pltpu.make_async_copy(fresh.at[slot], news.at[at_round, c, z], sem_own.at[3, slot]))
+            go(pltpu.make_async_copy(final.at[slot], grads.at[at_round], sem_own.at[4, slot]))
 
         def step(self):
             @pl.when(within(self.r - SLOTS))
@@ -206,23 +227,23 @@
             @pl.when(self.ok)
             def _():
                 slot, ring = lax.rem(self.r, SLOTS), lax.rem(self.r, RING)
-                tall = lax.rem(self.r, PER_TILE) >= 2 * CHIPS
+                at_round, _, kind, _ = plan(self.r)
                 total = on_chip(self.r, z) + line[z, ring].astype(F32) + line[CHIPS, ring].astype(F32)
                 final[slot] = total.astype(BF)
                 state(self.r, lambda d: d.wait())
 
-                @pl.when(tall)
+                @pl.when(kind == 2)
                 def _():
                     for i in range(D // LANE):
                         rows, cols = pl.ds(SUB * i, SUB), pl.ds(LANE * i, LANE)
                         fresh[slot, rows] = adamw(wdb[:, cols], mdb[:, cols], vdb[:, cols], final[slot, rows])
 
-                @pl.when(jnp.logical_not(tall))
+                @pl.when(kind < 2)
                 def _():
                     fresh[slot] = adamw(wb[...], mb[...], vb[...], final[slot])
 
-                self.outs(self.r, lambda d: d.start())
-                self.local(self.r, lambda d: d.start())
+                self.outs(self.r, lambda d: d.start(), at_round)
+                self.local(self.r, lambda d: d.start(), at_round)
 
             pl.when(within(self.r + 1))(lambda: state(self.r + 1, lambda d: d.start()))
 
@@ -236,32 +257,31 @@
             self.r, self.up = sent(k, self.zp), self.zp < z
             self.on = jnp.where(self.up, high, low)
 
-        def forward(self, r):
-            nxt, spot = jnp.where(self.up, z + 1, z - 1), news.at[r, c, self.zp]
+        def forward(self, r, at_round=0):
+            nxt, spot = jnp.where(self.up, z + 1, z - 1), news.at[at_round, c, self.zp]
             return remote(spot, spot, sem_ag_s.at[self.i, lax.rem(r, SLOTS)], sem_ag_r.at[self.zp, lax.rem(r, RING)], 2 * nxt + c)
 
-        def over(self, r):
-            return bundle(r, c, self.zp, sem_agp_s.at[self.i, lax.rem(lax.div(r, SLOTS), 2)])
+        def over(self, r, at_round=CHIPS - 1):
+            return bundle(r, at_round, c, self.zp, sem_agp_s.at[self.i, lax.rem(r, SLOTS)])
 
         def step(self):
-            old, now, last = within(self.r - SLOTS), within(self.r), lax.rem(self.r, SLOTS) == SLOTS - 1
-            pl.when(old & self.on)(lambda: self.forward(self.r - SLOTS).wait_send())
-            pl.when(old & last)(lambda: self.over(self.r - SLOTS).wait_send())
-            pl.when(now)(lambda: self.forward(self.r).wait_recv())
-            pl.when(now & self.on)(lambda: self.forward(self.r).start())
-            pl.when(now & last)(lambda: self.over(self.r).start())
-
-    def bundle(r, core, zp, send):
-        spot = news.at[pl.ds(r - (SLOTS - 1), SLOTS), core, zp]
-        return remote(spot, spot, send, sem_agp_r.at[zp, lax.rem(lax.div(r, SLOTS), SLOTS)], partner)
+            r, old, now = self.r, within(self.r - SLOTS), within(self.r)
+            pl.when(old & self.on)(lambda: self.forward(r - SLOTS).wait_send())
+            pl.when(old & ends_kind(r - SLOTS))(lambda: self.over(r - SLOTS).wait_send())
+
+            @pl.when(now)
+            def _():
+                self.forward(r).wait_recv()
+                at_round, _, _, q = plan(r)
+                pl.when(self.on)(lambda: self.forward(r, at_round).start())
+                pl.when(q == CHIPS - 1)(lambda: self.over(r, at_round).start())
+
+    def bundle(r, at_round, core, zp, send):
+        spot = news.at[pl.ds(at_round - (CHIPS - 1), CHIPS), core, zp]
+        return remote(spot, spot, send, sem_agp_r.at[zp, lax.rem(r, RING)], partner)
 
     def tick(k):
         pl.when(within(k - SLOTS))(lambda: pair(k - SLOTS).wait_send())
-
-        @pl.when(within(k))
-        def _():
-            pair(k).start()
-            own_terms(k).start()
 
         @pl.when(within(k - D0))
         def _():
@@ -274,19 +294,25 @@
             Gather(i, k).step()
         Own(k).step()
         r = sent(k, z) - LAGD
-        spot = news.at[r, 1 - c, z]
+        spot = news.at[0, 1 - c, z]
         pl.when(within(r))(lambda: remote(spot, spot, sem_agp_s.at[0, 0], sem_own_r.at[lax.rem(r, RING)], partner).wait_recv())
         for i in range(CHIPS - 1):
             zp = lax.rem(z + 1 + i, CHIPS)
             r = sent(k, zp) - LAGD
-            done = within(r) & (lax.rem(r, SLOTS) == SLOTS - 1)
-            pl.when(done)(lambda r=r, zp=zp: bundle(r, 1 - c, zp, sem_agp_s.at[0, 0]).wait_recv())
-
-    load_x.wait()
+            done = within(r) & ends_kind(r)
+            pl.when(done)(lambda r=r, zp=zp: bundle(r, CHIPS - 1, 1 - c, zp, sem_agp_s.at[0, 0]).wait_recv())
+
+    def begin_round(k):
+        @pl.when(within(k))
+        def _():
+            at_round = plan(k)[0]
+            pair(k, at_round).start()
+            own_terms(k, at_round).start()
+
     half = T // 2
-
-    @times(T // BLOCK)
-    def _(p):
+    blocks = half // BLOCK
+
+    def enter(p):
         rows = part(p, BLOCK)
         av[rows] = normed(xv[rows])
         dag[rows] = jnp.zeros((BLOCK, D), F32)
@@ -307,8 +333,20 @@
         slot, rows = lax.rem(lax.div(i, 2), 2), part(lax.rem(i, 2), half)
         dag[rows] = dag[rows] + dot(act[rows], wdt[slot])
 
+    def leave(p):
+        rows = part(p, BLOCK)
+        h = xv[rows] + dag[rows].astype(BF)
+        a = normed(h)
+        hv[rows], av[rows], at[:, rows] = h, a, a.T
+        dag[rows] = dau[rows] = jnp.zeros((BLOCK, D), F32)
+
+    load_x.wait()
+    times(blocks)(enter)
     tile_wait(0)
+    load_more.wait()
     hidden(0)
+    for p in range(blocks):
+        enter(blocks + p)
     load_dy.wait()
     turn(0)
 
@@ -322,14 +360,9 @@
         turn(i)
 
     back(2 * CHIPS - 1)
-
-    @times(T // BLOCK)
-    def _(p):
-        rows = part(p, BLOCK)
-        h = xv[rows] + dag[rows].astype(BF)
-        a = normed(h)
-        hv[rows], av[rows], at[:, rows] = h, a, a.T
-        dag[rows] = dau[rows] = jnp.zeros((BLOCK, D), F32)
+    for p in range(blocks):
+        leave(p)
+    times(2 * blocks, first=blocks)(leave)
 
     def next_layer(q):
         @times(PIECE // BLOCK)
@@ -344,11 +377,13 @@
             a = normed(xv[rows])
             ct[rows], ctt[:, rows], av[rows], at[:, rows] = by, by.T, a, a.T
 
-    def tokens(slot, p):
-        rows = part(p, PIECE)
-        a, by = av[rows], ct[rows]
-        for n in range(TILE // PIECE):
-            cols = pl.ds(PIECE * n, PIECE)
+    def tokens(slot, q):
+        cols = part(q, BLOCK)
+
+        @times(2)
+        def _(p):
+            rows = part(p, half)
+            a, by = av[rows], ct[rows]
             gate, up = dot(a, wgt[slot, :, cols]), dot(a, wut[slot, :, cols])
             dact = across(by, wdt[slot, cols]).astype(BF).astype(F32)
             sig = jax.nn.sigmoid(gate)
@@ -364,12 +399,12 @@
         for q in range(CHIPS):
             go(pltpu.make_async_copy(staged_d.at[q], terms.at[PER_TILE * t + 2 * CHIPS + q], sem_st.at[2 + q]))
 
-    def wide_terms(by, slot, q, r):
+    def wide_terms(by, kind, t, q):
         g = dot(at[...], by[:, part(q, BLOCK)]).astype(BF)
         for d in range(DEVICES):
             for s in range(2):
-                staged[slot, d % 2, d // 2, cut(s, ROWS)] = g[cut(d, ROWS), cut(s, LANE)]
-        put(slot, r).start()
+                staged[kind, d % 2, d // 2, cut(s, ROWS)] = g[cut(d, ROWS), cut(s, LANE)]
+        put(kind, PER_TILE * t + CHIPS * kind + q).start()
 
     def down_terms(i):
         g = dot(ctt[...], act[:, part(i, BLOCK)]).T.astype(BF)
@@ -378,46 +413,56 @@
                 for s in range(D // LANE):
                     staged_d[q, o, i, cut(s, SUB)] = g[cut(CHIPS * o + q, SUB), cut(s, LANE)]
 
-    def by_normed(to, by, w, slot, p):
-        rows = part(p, PIECE)
-        to[rows] = to[rows] + across(by[rows], w[slot])
+    def by_normed(slot, p, side):
+        rows, cols = part(p, PIECE), part(side, PIECE)
+        for to, by, w in ((dag, dgate, wgt), (dau, dup, wut)):
+            to[rows] = to[rows] + across(by[rows, cols], w[slot, :, cols])
 
     pl.semaphore_wait(barrier, 1 + low.astype(jnp.int32) + high.astype(jnp.int32))
 
-    @times(TICKS + AHEAD)
+    def makes(n):
+        _, i, early = stage(n)
+        odd = (i > CHIPS) & (lax.rem(i, 2) == 1)
+        real = (n >= CHIPS) & (n < ROUNDS)
+        return real & jnp.where(early, odd, lax.rem(i, 3) == 1), real & jnp.where(early, odd, lax.rem(i, 3) == 2)
+
+    @times(TICKS + AHEAD, first=CHIPS)
     def _(n):
-        q, phase, t = lax.rem(n, CHIPS), lax.div(lax.rem(n, PER_TILE), CHIPS), lax.div(n, PER_TILE)
+        t, i, early = stage(n)
         slot, busy = lax.rem(t, 2), n < ROUNDS
-
-        @pl.when(busy & (phase == 0) & (q == 0))
+        q = jnp.where(early, lax.div(jnp.maximum(i - CHIPS, 0), 2), lax.div(i, 3))
+        of_three = lax.rem(i, 3)
+        starts = jnp.where(early, (i >= CHIPS) & (lax.rem(i, 2) == 0), of_three == 0)
+        gate_terms, up_terms = makes(n)
+
+        @pl.when(busy & starts & (q == 0))
         def _():
             tile_wait(t)
-            pl.when(n < ROUNDS - PER_TILE)(lambda: tile(t + CHIPS + 1))
-
-        pl.when((n > 0) & (n <= ROUNDS) & (lax.rem(n - 1, PER_TILE) >= CHIPS))(lambda: put(lax.rem(n - 1, 2), n - 1 - CHIPS).wait())
-        pl.when((phase == 0) & (q == 2) & (n >= PER_TILE) & (n < ROUNDS + PER_TILE))(lambda: put_d(t - 1, lambda d: d.wait()))
-
-        def work():
-            @pl.when(busy & (phase == 0))
-            def _():
-                pl.when(t == CHIPS)(lambda: next_layer(q))
-                tokens(slot, q)
-
-            @pl.when(busy & (phase == 1))
-            def _():
-                wide_terms(dgate, lax.rem(n, 2), q, n - CHIPS)
-                pl.when((t > 0) & (t < CHIPS))(lambda: by_normed(dag, dgate, wgt, slot, q))
-
-            @pl.when(busy & (phase == 2))
-            def _():
-                wide_terms(dup, lax.rem(n, 2), q, n - CHIPS)
-                down_terms(q)
-                pl.when(t == 0)(lambda: by_normed(dag, dgate, wgt, slot, q))
-                pl.when(t < CHIPS)(lambda: by_normed(dau, dup, wut, slot, q))
-                pl.when(q == CHIPS - 1)(lambda: put_d(t, lambda d: d.start()))
+
+        pl.when((i == CHIPS + 2) & (n < ROUNDS - PER_TILE))(lambda: tile(t + CHIPS + 1))
 
         tick(n - AHEAD)
-        work()
+
+        for number, made in enumerate(makes(n - 1)):
+            pl.when(made)(lambda number=number: put(number, 0).wait())
+        pl.when((i == 1) & (n >= PER_TILE) & (n < ROUNDS + PER_TILE))(lambda: put_d(0, lambda d: d.wait()))
+        begin_round(n - AHEAD)
+
+        first_tile, turning = t == 0, t == CHIPS
+        between = (t > 0) & (t < CHIPS) & (of_three > 0)
+        back_on = first_tile & (i >= 2 * CHIPS) | turning & (i < CHIPS) | between
+        before = turning | ~first_tile & (q < 2)
+        place = jnp.where(first_tile, i - 2 * CHIPS, jnp.where(turning, i, 2 * lax.rem(q, 2) + of_three - 1))
+        pl.when(back_on)(lambda: by_normed(jnp.where(before, 1 - slot, slot), place, before.astype(jnp.int32)))
+        pl.when(turning & (i < CHIPS))(lambda: next_layer(i))
+        pl.when(busy & starts)(lambda: tokens(slot, q))
+        pl.when(gate_terms)(lambda: wide_terms(dgate, 0, t, q))
+
+        @pl.when(up_terms)
+        def _():
+            wide_terms(dup, 1, t, q)
+            down_terms(q)
+            pl.when(q == CHIPS - 1)(lambda: put_d(t, lambda d: d.start()))
 
 
 def backward(x, dy, weights, m, v):
@@ -447,8 +492,8 @@
             bf(T, TILE), bf(T, TILE), bf(T, TILE), f32(T, D), f32(T, D),
             bf(2, 2, CHIPS, *message), bf(CHIPS, 2, CHIPS, *message),
             dma(SLOTS), dma(KEPT), dma(3, SLOTS), dma(CHIPS + 1, RING), dma(KEPT), dma(3, 2), dma(5, SLOTS),
-            dma(3, SLOTS), dma(CHIPS, RING), dma(3, 2), dma(CHIPS, SLOTS), dma(RING),
-            dma(2), dma(3, 2), dma(2 + CHIPS),
+            dma(3, SLOTS), dma(CHIPS, RING), dma(3, SLOTS), dma(CHIPS, RING), dma(RING),
+            dma(3), dma(3, 2), dma(2 + CHIPS),
         ],
         compiler_params=pltpu.CompilerParams(collective_id=0, has_side_effects=True, vmem_limit_bytes=67_043_328),
     )(x, dy, *weights, *m, *v)

time: 488 us -> 466 us (0.955)
  Pallas kernels: 487 us -> 465 us
    pallas_call x1, Pallas kernels: 454 us -> 431 us  [backward(): pl.pallas_call(kernel, name='backward', out_shape=[jax.ShapeDtypeStruct((...]
where the time goes in v3:
time: 466 us
  Pallas kernels  465 us (100%)
    pallas_call x1, Pallas kernels, backward(): pl.pallas_call(kernel, name='backward', out_shape=[jax.ShapeDtypeStruct((...  431 us
    pallas_call x1, Pallas kernels, finish(): pl.pallas_call(finish_kernel, name='finish', out_shape=[*[jax.ShapeDtypeS...  33.6 us

profile of v3, /device:TPU:0, one launch (start us, length us, event | category | flops | bytes accessed | tf_op | source)
XLA Modules:
  0.0 465.6 jit_solution(17698446152191382801)
XLA Ops:
  0.6 431.2 %backward.1 = (bf16[96,2,4,160,128]{4,3,2,1,0:T(8,128)(2,1)}, bf16[96,160,128]{2,1,0:T(8,128)(2,1)}, bf16[96,2,4,160,128]{4,3,2,1,0:T(8,128)(2,1)}) custom-call(bf16[2048,640]{1,0:T(8,128)(2,1)} %bitcast.6, bf16[2048,640]{1,0:T(8,128)(2,1)} %bitcast.7, bf16[2,640,4096]{2,1,0:T(8,128)(2,1)} %w_g.1, bf16[2,640,4096]{2,1,0:T(8,128)(2,1)} %w_u.1, ...), custom_call_target="tpu_custom_call" | custom-call | tf_op jit(solution)/shard_map/backward/pallas_call | solution.py:481
  431.9 33.6 %finish.1 = (bf16[2,640,4096]{2,1,0:T(8,128)(2,1)}, bf16[2,640,4096]{2,1,0:T(8,128)(2,1)}, bf16[2,4096,640]{2,1,0:T(8,128)(2,1)}, f32[2,80,4096]{2,1,0:T(8,128)}...) custom-call(bf16[2,4,3,4,2,4,160,128]{7,6,5,4,3,2,1,0:T(8,128)(2,1)}, ...), custom_call_target="tpu_custom_call" | custom-call | tf_op jit(solution)/shard_map/finish/pallas_call | solution.py:590

commit v4 on v3

--- a/solution.py
+++ b/solution.py
@@ -13,10 +13,11 @@
 TILE = DEVICES * LANE
 ROWS, TALL = D // DEVICES, FF // DEVICES
 PIECE, BLOCK = 512, 256
+PARTS = 2
 
 ROUNDS, MR, SUB = 96, 160, 32
 PER_TILE = 12
-D0, LAG, LAGF, LAGA, LAGD = 2, 2, 3, 3, 2
+D0, LAG, LAGF, LAGA, LAGD = 1, 2, 2, 2, 2
 RING, SLOTS, KEPT = 16, 4, 12
 TICKS = ROUNDS + D0 + 3 * LAG + LAGF + 2 * LAGA + max(LAGD, SLOTS)
 AHEAD = 6
@@ -96,6 +97,11 @@
             pltpu.make_async_copy(w_u.at[of, :, cols], wut.at[slot, :, to], sems[1]).start()
             pltpu.make_async_copy(w_d.at[of, cols], wdt.at[slot, to], sems[2]).start()
 
+    def plain_tile(t):
+        slot, cols = lax.rem(t, 2), part(t, TILE)
+        for i, (src, dst) in enumerate(((w_g.at[0, :, cols], wgt), (w_u.at[0, :, cols], wut), (w_d.at[0, cols], wdt))):
+            pltpu.make_async_copy(src, dst.at[slot], sem_w.at[i, slot]).start()
+
     def tile_wait(t):
         slot, all_of = lax.rem(t, 2), pl.ds(0, TILE)
         sems = [sem_w.at[i, slot] for i in range(3)]
@@ -103,16 +109,16 @@
         pltpu.make_async_copy(w_u.at[0, :, all_of], wut.at[slot], sems[1]).wait()
         pltpu.make_async_copy(w_d.at[0, all_of], wdt.at[slot], sems[2]).wait()
 
-    line[...] = jnp.zeros_like(line)
     upper, lower = pl.ds(0, T // 2), pl.ds(T // 2, T // 2)
     load_x, load_more = (pltpu.make_async_copy(x.at[rows], xv.at[rows], sem_in.at[i]) for i, rows in enumerate((upper, lower)))
     load_dy = pltpu.make_async_copy(dy, ct, sem_in.at[2])
     load_x.start()
-    tile(0)
+    plain_tile(0)
     load_more.start()
     load_dy.start()
-    tile(1)
-
+    plain_tile(1)
+
+    line[...] = jnp.zeros_like(line)
     me = lax.axis_index("dp")
     z, c = lax.div(me, 2), lax.rem(me, 2)
     partner = me + 1 - 2 * c
@@ -289,9 +295,9 @@
             own_terms(k - D0).wait()
 
         for i in range(CHIPS - 1):
+            Gather(i, k).step()
+        for i in range(CHIPS - 1):
             Line(i, k).step()
-        for i in range(CHIPS - 1):
-            Gather(i, k).step()
         Own(k).step()
         r = sent(k, z) - LAGD
         spot = news.at[0, 1 - c, z]
@@ -317,8 +323,8 @@
         av[rows] = normed(xv[rows])
         dag[rows] = jnp.zeros((BLOCK, D), F32)
 
-    def hidden(i):
-        slot, rows = lax.rem(lax.div(i, 2), 2), part(lax.rem(i, 2), half)
+    def hidden(t, p):
+        slot, rows = lax.rem(t, 2), pl.ds(half * p, half)
         a = av[rows]
         for n in range(TILE // PIECE):
             cols = pl.ds(PIECE * n, PIECE)
@@ -329,9 +335,9 @@
         rows = part(i, BLOCK)
         ctt[:, rows] = ct[rows].T
 
-    def back(i):
-        slot, rows = lax.rem(lax.div(i, 2), 2), part(lax.rem(i, 2), half)
-        dag[rows] = dag[rows] + dot(act[rows], wdt[slot])
+    def back(t, p, n=half):
+        rows = pl.ds(n * p, n)
+        dag[rows] = dag[rows] + dot(act[rows], wdt[lax.rem(t, 2)])
 
     def leave(p):
         rows = part(p, BLOCK)
@@ -344,25 +350,32 @@
     times(blocks)(enter)
     tile_wait(0)
     load_more.wait()
-    hidden(0)
+    hidden(0, 0)
     for p in range(blocks):
         enter(blocks + p)
     load_dy.wait()
     turn(0)
-
-    @times(2 * CHIPS, first=1)
-    def _(i):
-        first, t = lax.rem(i, 2) == 0, lax.div(i, 2)
-        pl.when(first)(lambda: tile_wait(t))
-        pl.when(jnp.logical_not(first) & (t > 0))(lambda: tile(t + 1))
-        back(i - 1)
-        hidden(i)
-        turn(i)
-
-    back(2 * CHIPS - 1)
-    for p in range(blocks):
-        leave(p)
-    times(2 * blocks, first=blocks)(leave)
+    back(0, 0)
+    hidden(0, 1)
+    turn(1)
+
+    @times(CHIPS, first=1)
+    def _(t):
+        tile_wait(t)
+        back(t - 1, 1)
+        hidden(t, 0)
+        turn(2 * t)
+        pl.when(t < CHIPS - 1)(lambda: plain_tile(t + 1))
+        pl.when(t == CHIPS - 1)(lambda: tile(t + 1))
+        back(t, 0)
+        hidden(t, 1)
+        turn(2 * t + 1)
+
+    for third in range(2):
+        back(CHIPS - 1, 2 + third, PIECE)
+        for p in range(3):
+            leave(3 * third + p)
+    times(2 * blocks, first=2 * blocks - 2)(leave)
 
     def next_layer(q):
         @times(PIECE // BLOCK)
@@ -379,10 +392,8 @@
 
     def tokens(slot, q):
         cols = part(q, BLOCK)
-
-        @times(2)
-        def _(p):
-            rows = part(p, half)
+        for p in range(PARTS):
+            rows = pl.ds(T // PARTS * p, T // PARTS)
             a, by = av[rows], ct[rows]
             gate, up = dot(a, wgt[slot, :, cols]), dot(a, wut[slot, :, cols])
             dact = across(by, wdt[slot, cols]).astype(BF).astype(F32)
@@ -392,19 +403,22 @@
             dup[rows, cols] = (dact * silu).astype(BF)
             dgate[rows, cols] = (dact * up * (sig + silu * (1.0 - sig))).astype(BF)
 
-    def put(slot, r):
-        return pltpu.make_async_copy(staged.at[slot], terms.at[r], sem_st.at[slot])
+    def put(kind, r):
+        return pltpu.make_async_copy(staged.at[kind], terms.at[r], sem_st.at[kind])
 
     def put_d(t, go):
         for q in range(CHIPS):
             go(pltpu.make_async_copy(staged_d.at[q], terms.at[PER_TILE * t + 2 * CHIPS + q], sem_st.at[2 + q]))
 
-    def wide_terms(by, kind, t, q):
+    def wide_terms(by, kind, q):
         g = dot(at[...], by[:, part(q, BLOCK)]).astype(BF)
         for d in range(DEVICES):
             for s in range(2):
                 staged[kind, d % 2, d // 2, cut(s, ROWS)] = g[cut(d, ROWS), cut(s, LANE)]
-        put(kind, PER_TILE * t + CHIPS * kind + q).start()
+
+    def puts(t, q):
+        for kind in range(2):
+            put(kind, PER_TILE * t + CHIPS * kind + q).start()
 
     def down_terms(i):
         g = dot(ctt[...], act[:, part(i, BLOCK)]).T.astype(BF)
@@ -413,18 +427,17 @@
                 for s in range(D // LANE):
                     staged_d[q, o, i, cut(s, SUB)] = g[cut(CHIPS * o + q, SUB), cut(s, LANE)]
 
-    def by_normed(slot, p, side):
-        rows, cols = part(p, PIECE), part(side, PIECE)
-        for to, by, w in ((dag, dgate, wgt), (dau, dup, wut)):
-            to[rows] = to[rows] + across(by[rows, cols], w[slot, :, cols])
+    sides = ((dag, dgate, wgt), (dau, dup, wut))
+
+    def by_normed(which, slot, rows, side):
+        (to, by, w), cols = sides[which], part(side, PIECE)
+        to[rows] = to[rows] + across(by[rows, cols], w[slot, :, cols])
 
     pl.semaphore_wait(barrier, 1 + low.astype(jnp.int32) + high.astype(jnp.int32))
 
     def makes(n):
         _, i, early = stage(n)
-        odd = (i > CHIPS) & (lax.rem(i, 2) == 1)
-        real = (n >= CHIPS) & (n < ROUNDS)
-        return real & jnp.where(early, odd, lax.rem(i, 3) == 1), real & jnp.where(early, odd, lax.rem(i, 3) == 2)
+        return (n >= CHIPS) & (n < ROUNDS) & jnp.where(early, (i > CHIPS) & (lax.rem(i, 2) == 1), lax.rem(i, 3) == 1)
 
     @times(TICKS + AHEAD, first=CHIPS)
     def _(n):
@@ -433,7 +446,6 @@
         q = jnp.where(early, lax.div(jnp.maximum(i - CHIPS, 0), 2), lax.div(i, 3))
         of_three = lax.rem(i, 3)
         starts = jnp.where(early, (i >= CHIPS) & (lax.rem(i, 2) == 0), of_three == 0)
-        gate_terms, up_terms = makes(n)
 
         @pl.when(busy & starts & (q == 0))
         def _():
@@ -443,26 +455,59 @@
 
         tick(n - AHEAD)
 
-        for number, made in enumerate(makes(n - 1)):
-            pl.when(made)(lambda number=number: put(number, 0).wait())
+        @pl.when(makes(n - 1))
+        def _():
+            put(0, 0).wait()
+            put(1, 0).wait()
+
         pl.when((i == 1) & (n >= PER_TILE) & (n < ROUNDS + PER_TILE))(lambda: put_d(0, lambda d: d.wait()))
         begin_round(n - AHEAD)
 
-        first_tile, turning = t == 0, t == CHIPS
-        between = (t > 0) & (t < CHIPS) & (of_three > 0)
-        back_on = first_tile & (i >= 2 * CHIPS) | turning & (i < CHIPS) | between
-        before = turning | ~first_tile & (q < 2)
-        place = jnp.where(first_tile, i - 2 * CHIPS, jnp.where(turning, i, 2 * lax.rem(q, 2) + of_three - 1))
-        pl.when(back_on)(lambda: by_normed(jnp.where(before, 1 - slot, slot), place, before.astype(jnp.int32)))
-        pl.when(turning & (i < CHIPS))(lambda: next_layer(i))
+        ends = busy & ~early & (of_three == 2)
+        inner, turning = t < CHIPS, (t == CHIPS) & (i < CHIPS)
+        before = q < 2
+        share = (jnp.where(before, 1 - slot, slot), part(lax.rem(q, 2), half), before.astype(jnp.int32))
+        own_share = (slot, part(lax.div(i - 2 * CHIPS, 2), half), 0)
+        late = (t == 0) & (i >= 2 * CHIPS)
+
+        @pl.when(turning)
+        def _():
+            for which in range(2):
+                by_normed(which, 1 - slot, part(i, PIECE), 1)
+            next_layer(i)
+
         pl.when(busy & starts)(lambda: tokens(slot, q))
-        pl.when(gate_terms)(lambda: wide_terms(dgate, 0, t, q))
-
-        @pl.when(up_terms)
-        def _():
-            wide_terms(dup, 1, t, q)
+
+        @pl.when(makes(n) & early)
+        def _():
+            wide_terms(dgate, 0, q)
+            wide_terms(dup, 1, q)
             down_terms(q)
-            pl.when(q == CHIPS - 1)(lambda: put_d(t, lambda d: d.start()))
+            puts(t, q)
+
+        for which in range(2):
+            pl.when(late & (lax.rem(i, 2) == which))(lambda which=which: by_normed(which, *own_share))
+
+        @pl.when(makes(n) & ~early & inner)
+        def _():
+            wide_terms(dgate, 0, q)
+            wide_terms(dup, 1, q)
+            by_normed(0, *share)
+            puts(t, q)
+
+        @pl.when(makes(n) & ~early & ~inner)
+        def _():
+            wide_terms(dgate, 0, q)
+            wide_terms(dup, 1, q)
+            puts(t, q)
+
+        @pl.when(ends & inner)
+        def _():
+            down_terms(q)
+            by_normed(1, *share)
+
+        pl.when(ends & ~inner)(lambda: down_terms(q))
+        pl.when(busy & (i == PER_TILE - 1))(lambda: put_d(t, lambda d: d.start()))
 
 
 def backward(x, dy, weights, m, v):
@@ -524,7 +569,7 @@
         core, chip, of = lax.rem(d, 2), lax.div(d, 2), 1 - n
         for kind in range(3):
             if kind < 2:
-                grad = grads.at[of, :, kind, chip]
+                grad = grads.at[of, :, kind, chip, part(core, ROWS)]
             else:
                 grad = grads.at[of, chip, kind, pl.ds(2 * core, 2)]
             pairs = (
@@ -554,7 +599,7 @@
 
     @times(steps)
     def _(i):
-        slot, to, s = lax.rem(i, DEPTH), lax.rem(i, STORES), lax.rem(i, 2)
+        slot, to = lax.rem(i, DEPTH), lax.rem(i, STORES)
         loads(i, lambda d: d.wait())
         pl.when(i >= STORES)(lambda: stores(i - STORES, lambda d: d.wait()))
 
@@ -567,7 +612,7 @@
                 for q in range(CHIPS):
                     for half in range(2):
                         w_to[kind][to, :, cut(4 * (2 * q + half) + j, LANE)] = new_in[kind][slot, j, q, cut(half, ROWS)]
-                step(kind, slice(ROWS), cut(j, LANE), grad_in[kind][slot, j, part(s, ROWS)])
+                step(kind, slice(ROWS), cut(j, LANE), grad_in[kind][slot, j])
         for number in range(D // LANE):
             for j in range(CHIPS):
                 for q in range(CHIPS):
@@ -595,7 +640,7 @@
         out_specs=[anywhere] * 9,
         scratch_shapes=[
             *[pltpu.VMEM((DEPTH, CHIPS, CHIPS, MR, LANE), BF)] * 3,
-            *[pltpu.VMEM((DEPTH, n, MR, LANE), BF) for n in (CHIPS, CHIPS, 2)],
+            *[pltpu.VMEM((DEPTH, *b, LANE), BF) for b in ((CHIPS, ROWS), (CHIPS, ROWS), (2, MR))],
             *[pltpu.VMEM((DEPTH, *b), F32) for b in blocks * 2],
             *[pltpu.VMEM((STORES, *b), BF) for b in ((ROWS, FF), (ROWS, FF), (TALL, D))],
             *[pltpu.VMEM((STORES, *b), F32) for b in blocks * 2],

time: 466 us -> 462 us (level)
  no operation moved by 1% of the time
where the time goes in v4:
time: 462 us; the launch traced here: 461 us
  Pallas kernels  461 us (100%)
    pallas_call x1, Pallas kernels, backward(): pl.pallas_call(kernel, name='backward', out_shape=[jax.ShapeDtypeStruct((...  427 us
    pallas_call x1, Pallas kernels, finish(): pl.pallas_call(finish_kernel, name='finish', out_shape=[*[jax.ShapeDtypeS...  34 us

profile of v4, /device:TPU:0, one launch (start us, length us, event | category | flops | bytes accessed | tf_op | source)
XLA Modules:
  0.0 461.4 jit_solution(17105562885542355233)
XLA Ops:
  0.6 426.6 %backward.1 = (bf16[96,2,4,160,128]{4,3,2,1,0:T(8,128)(2,1)}, bf16[96,160,128]{2,1,0:T(8,128)(2,1)}, bf16[96,2,4,160,128]{4,3,2,1,0:T(8,128)(2,1)}) custom-call(bf16[2048,640]{1,0:T(8,128)(2,1)} %bitcast.6, bf16[2048,640]{1,0:T(8,128)(2,1)} %bitcast.7, bf16[2,640,4096]{2,1,0:T(8,128)(2,1)} %w_g.1, bf16[2,640,4096]{2,1,0:T(8,128)(2,1)} %w_u.1, ...), custom_call_target="tpu_custom_call" | custom-call | tf_op jit(solution)/shard_map/backward/pallas_call | solution.py:526
  427.3 34.0 %finish.1 = (bf16[2,640,4096]{2,1,0:T(8,128)(2,1)}, bf16[2,640,4096]{2,1,0:T(8,128)(2,1)}, bf16[2,4096,640]{2,1,0:T(8,128)(2,1)}, f32[2,80,4096]{2,1,0:T(8,128)}...) custom-call(bf16[2,4,3,4,2,4,160,128]{7,6,5,4,3,2,1,0:T(8,128)(2,1)}, ...), custom_call_target="tpu_custom_call" | custom-call | tf_op jit(solution)/shard_map/finish/pallas_call | solution.py:635

commit v5 on v4

--- a/solution.py
+++ b/solution.py
@@ -14,6 +14,7 @@
 ROWS, TALL = D // DEVICES, FF // DEVICES
 PIECE, BLOCK = 512, 256
 PARTS = 2
+KEEP = 2 * 3 * T * TILE + 2 * 2 * D * T + 4 * T * D
 
 ROUNDS, MR, SUB = 96, 160, 32
 PER_TILE = 12
@@ -82,11 +83,11 @@
 
 def kernel(
     x, dy, w_g, w_u, w_d, m_g, m_u, m_d, v_g, v_u, v_d,
-    news, grads, terms,
+    news, grads, terms, act, dgate, dup, dag, at, ctt,
     mine, others, line, summed, fresh, final, wb, mb, vb, wdb, mdb, vdb,
-    hv, xv, av, at, ct, ctt, wgt, wut, wdt, act, dgate, dup, dag, dau, staged, staged_d,
+    hv, xv, av, ct, wgt, wut, wdt, dau, staged, staged_d,
     sem_pair_s, sem_pair_r, sem_line_s, sem_line_r, sem_mine, sem_state, sem_own, sem_ag_s, sem_ag_r, sem_agp_s, sem_agp_r, sem_own_r,
-    sem_in, sem_w, sem_st,
+    sem_in, sem_w, sem_st, sem_keep,
 ):
     def tile(t):
         slot, of, j = lax.rem(t, 2), lax.rem(lax.div(t, CHIPS), 2), lax.rem(t, CHIPS)
@@ -435,6 +436,37 @@
 
     pl.semaphore_wait(barrier, 1 + low.astype(jnp.int32) + high.astype(jnp.int32))
 
+    def states_kept(go):
+        for i, src in enumerate((m_d, v_d)):
+            for of in range(2):
+                place = 2 * i + of
+                go(pltpu.make_async_copy(src.at[of], dag.at[cut(place, TALL)], sem_keep.at[5 + place]))
+
+    def keep(e):
+        d, kind = lax.div(e, 2), lax.rem(e, 2)
+        core, chip = lax.rem(d, 2), lax.div(d, 2)
+        pl.when(e == 0)(lambda: states_kept(lambda c: c.start()))
+
+        def take(j, q, kind, buf, row, col, number):
+            to = buf.at[pl.ds(pl.multiple_of(MR * row, MR), MR), cut(col, LANE)]
+            pltpu.make_async_copy(news.at[PER_TILE * j + CHIPS * kind + q, core, chip], to, sem_keep.at[number]).start()
+
+        for number, buf in enumerate((act, dgate, dup)):
+
+            @pl.when(lax.div(d, 3) == number)
+            def _(number=number, buf=buf):
+                for j in range(CHIPS):
+                    for q in range(CHIPS):
+                        take(j, q, kind, buf, CHIPS * lax.rem(d, 3) + 2 * kind + j // 2, CHIPS * (j % 2) + q, number)
+
+        for number, buf in enumerate((at, ctt)):
+
+            @pl.when((kind == 0) & (lax.div(d, CHIPS) == number))
+            def _(number=number, buf=buf):
+                for j in range(CHIPS):
+                    for q in range(CHIPS):
+                        take(j, q, 2, buf, lax.rem(d, CHIPS), CHIPS * j + q, 3 + number)
+
     def makes(n):
         _, i, early = stage(n)
         return (n >= CHIPS) & (n < ROUNDS) & jnp.where(early, (i > CHIPS) & (lax.rem(i, 2) == 1), lax.rem(i, 3) == 1)
@@ -508,6 +540,16 @@
 
         pl.when(ends & ~inner)(lambda: down_terms(q))
         pl.when(busy & (i == PER_TILE - 1))(lambda: put_d(t, lambda d: d.start()))
+        pl.when((n >= ROUNDS) & (n < ROUNDS + 2 * DEVICES))(lambda: keep(n - ROUNDS))
+
+    states_kept(lambda d: d.wait())
+    for number, rounds in enumerate((PER_TILE, PER_TILE, DEVICES, DEVICES, DEVICES)):
+        some = pl.ds(0, rounds)
+        pltpu.make_async_copy(news.at[some], terms.at[some], sem_keep.at[number]).wait()
+
+
+def in_hbm(arrays):
+    return [pltpu.with_memory_space_constraint(a, pltpu.HBM) for a in arrays]
 
 
 def backward(x, dy, weights, m, v):
@@ -522,29 +564,29 @@
 
     message = (MR, LANE)
     outs = ((2, CHIPS, *message), message, (2, CHIPS, *message))
-    anywhere = pl.BlockSpec(memory_space=pl.ANY)
+    anywhere = pl.BlockSpec(memory_space=pltpu.HBM)
     return pl.pallas_call(
         kernel,
         name="backward",
-        out_shape=[jax.ShapeDtypeStruct((ROUNDS, *s), BF) for s in outs],
+        out_shape=[*[jax.ShapeDtypeStruct((ROUNDS, *s), BF) for s in outs], bf(T, TILE), bf(T, TILE), bf(T, TILE), f32(T, D), bf(D, T), bf(D, T)],
         in_specs=[anywhere] * 11,
-        out_specs=[anywhere] * len(outs),
+        out_specs=[anywhere] * len(outs) + [pl.BlockSpec(memory_space=pltpu.VMEM)] * 6,
         scratch_shapes=[
             bf(KEPT, CHIPS, *message), bf(KEPT, CHIPS, *message), bf(CHIPS + 1, RING, *message), bf(3, SLOTS, *message), bf(SLOTS, *message), bf(SLOTS, *message),
             bf(*message), f32(*message), f32(*message), bf(SUB, D), f32(SUB, D), f32(SUB, D),
-            bf(T, D), bf(T, D), bf(T, D), bf(D, T), bf(T, D), bf(D, T),
+            bf(T, D), bf(T, D), bf(T, D), bf(T, D),
             bf(2, D, TILE), bf(2, D, TILE), bf(2, TILE, D),
-            bf(T, TILE), bf(T, TILE), bf(T, TILE), f32(T, D), f32(T, D),
+            f32(T, D),
             bf(2, 2, CHIPS, *message), bf(CHIPS, 2, CHIPS, *message),
             dma(SLOTS), dma(KEPT), dma(3, SLOTS), dma(CHIPS + 1, RING), dma(KEPT), dma(3, 2), dma(5, SLOTS),
             dma(3, SLOTS), dma(CHIPS, RING), dma(3, SLOTS), dma(CHIPS, RING), dma(RING),
-            dma(3), dma(3, 2), dma(2 + CHIPS),
+            dma(3), dma(3, 2), dma(2 + CHIPS), dma(9),
         ],
-        compiler_params=pltpu.CompilerParams(collective_id=0, has_side_effects=True, vmem_limit_bytes=67_043_328),
-    )(x, dy, *weights, *m, *v)
-
-
-DEPTH, STORES = 4, 3
+        compiler_params=pltpu.CompilerParams(collective_id=0, has_side_effects=True, vmem_limit_bytes=67_043_328 - KEEP),
+    )(*in_hbm((x, dy, *weights, *m, *v)))
+
+
+DEPTH, STORES = 3, 2
 
 
 def finish_kernel(*refs):
@@ -552,14 +594,15 @@
         return refs[first : first + 3]
 
     news, grads, m, v = refs[0], refs[1], three(2), three(5)
-    w_out, m_out, v_out = three(8), three(11), three(14)
-    new_in, grad_in, m_in, v_in = three(17), three(20), three(23), three(26)
-    w_to, m_to, v_to = three(29), three(32), three(35)
-    sem_in, sem_out = refs[38:]
+    act, dgate, dup, dag, at, ctt = refs[8:14]
+    w_out, m_out, v_out = three(14), three(17), three(20)
+    new_in, grad_in, m_in, v_in = three(23), three(26), refs[29:31], refs[31:33]
+    w_to, m_to, v_to = three(33), three(36), three(39)
+    sem_in, sem_out = refs[42:]
     steps = 2 * DEVICES
 
     def where(i):
-        n, d = lax.div(i, DEVICES), lax.rem(i, DEVICES)
+        n, d = 1 - lax.rem(i, 2), lax.div(i, 2)
         wide, tall = pl.ds(pl.multiple_of(PIECE * d, PIECE), PIECE), pl.ds(pl.multiple_of(2 * SUB * d, 2 * SUB), 2 * SUB)
         return n, d, [(n, slice(None), wide)] * 2 + [(n, tall)]
 
@@ -569,17 +612,16 @@
         core, chip, of = lax.rem(d, 2), lax.div(d, 2), 1 - n
         for kind in range(3):
             if kind < 2:
-                grad = grads.at[of, :, kind, chip, part(core, ROWS)]
+                pairs = [(grads.at[of, :, kind, chip], grad_in[kind]), (m[kind].at[states[kind]], m_in[kind]), (v[kind].at[states[kind]], v_in[kind])]
             else:
-                grad = grads.at[of, chip, kind, pl.ds(2 * core, 2)]
-            pairs = (
-                (news.at[of, :, kind, :, core, chip], new_in[kind]),
-                (grad, grad_in[kind]),
-                (m[kind].at[states[kind]], m_in[kind]),
-                (v[kind].at[states[kind]], v_in[kind]),
-            )
+                pairs = [(grads.at[of, chip, kind, pl.ds(2 * core, 2)], grad_in[kind])]
             for number, (src, dst) in enumerate(pairs):
                 go(pltpu.make_async_copy(src, dst.at[slot], sem_in.at[slot, kind, number]))
+
+        @pl.when(n == 0)
+        def _():
+            for kind in range(3):
+                go(pltpu.make_async_copy(news.at[of, :, kind, :, core, chip], new_in[kind].at[slot], sem_in.at[slot, kind, 3]))
 
     def stores(i, go):
         slot = lax.rem(i, STORES)
@@ -600,61 +642,99 @@
     @times(steps)
     def _(i):
         slot, to = lax.rem(i, DEPTH), lax.rem(i, STORES)
-        loads(i, lambda d: d.wait())
-        pl.when(i >= STORES)(lambda: stores(i - STORES, lambda d: d.wait()))
-
-        def step(kind, rows, cols, g):
-            old_m, old_v = m_in[kind][slot, rows, cols], v_in[kind][slot, rows, cols]
-            m_to[kind][to, rows, cols], v_to[kind][to, rows, cols] = moments(old_m, old_v, g.astype(F32))
-
-        for kind in range(2):
+        n, d, _ = where(i)
+        loads(i, lambda c: c.wait())
+        pl.when(i >= STORES)(lambda: stores(i - STORES, lambda c: c.wait()))
+
+        def wide(kind, message):
             for j in range(CHIPS):
                 for q in range(CHIPS):
                     for half in range(2):
-                        w_to[kind][to, :, cut(4 * (2 * q + half) + j, LANE)] = new_in[kind][slot, j, q, cut(half, ROWS)]
-                step(kind, slice(ROWS), cut(j, LANE), grad_in[kind][slot, j])
+                        w_to[kind][to, :, cut(4 * (2 * q + half) + j, LANE)] = message(j, q, half)
+
+        def tall(message):
+            for number in range(D // LANE):
+                for j in range(CHIPS):
+                    for q in range(CHIPS):
+                        w_to[2][to, cut(CHIPS * j + q, SUB), cut(number, LANE)] = message(j, q, number)
+
+        @pl.when(n == 0)
+        def _():
+            for kind in range(2):
+                wide(kind, lambda j, q, half, kind=kind: new_in[kind][slot, j, q, cut(half, ROWS)])
+            tall(lambda j, q, number: new_in[2][slot, j, q, cut(number, SUB)])
+
+        for place, buf in enumerate((act, dgate, dup)):
+
+            @pl.when((n == 1) & (lax.div(d, 3) == place))
+            def _(buf=buf):
+                for kind in range(2):
+
+                    def message(j, q, half, kind=kind):
+                        row = MR * (CHIPS * lax.rem(d, 3) + 2 * kind + j // 2) + ROWS * half
+                        return buf[pl.ds(pl.multiple_of(row, 16), ROWS), cut(CHIPS * (j % 2) + q, LANE)]
+
+                    wide(kind, message)
+
+        for place, buf in enumerate((at, ctt)):
+
+            @pl.when((n == 1) & (lax.div(d, CHIPS) == place))
+            def _(buf=buf):
+                def message(j, q, number):
+                    return buf[pl.ds(pl.multiple_of(MR * lax.rem(d, CHIPS) + SUB * number, SUB), SUB), cut(CHIPS * j + q, LANE)]
+
+                tall(message)
+
+        s = lax.rem(d, 2)
+        for kind in range(2):
+            for j in range(CHIPS):
+                cols = cut(j, LANE)
+                old_m, old_v = m_in[kind][slot, :, cols], v_in[kind][slot, :, cols]
+                g = grad_in[kind][slot, j, part(s, ROWS)].astype(F32)
+                m_to[kind][to, :, cols], v_to[kind][to, :, cols] = moments(old_m, old_v, g)
         for number in range(D // LANE):
-            for j in range(CHIPS):
-                for q in range(CHIPS):
-                    w_to[2][to, cut(CHIPS * j + q, SUB), cut(number, LANE)] = new_in[2][slot, j, q, cut(number, SUB)]
             for q in range(2):
-                step(2, cut(q, SUB), cut(number, LANE), grad_in[2][slot, q, cut(number, SUB)])
-        stores(i, lambda d: d.start())
-        pl.when(i < steps - DEPTH)(lambda: loads(i + DEPTH, lambda d: d.start()))
+                cols, row = cut(number, LANE), TALL * n + 2 * SUB * d + SUB * q
+                old_m = dag[pl.ds(pl.multiple_of(row, SUB), SUB), cols]
+                old_v = dag[pl.ds(pl.multiple_of(row + 2 * TALL, SUB), SUB), cols]
+                g = grad_in[2][slot, q, cut(number, SUB)].astype(F32)
+                m_to[2][to, cut(q, SUB), cols], v_to[2][to, cut(q, SUB), cols] = moments(old_m, old_v, g)
+        stores(i, lambda c: c.start())
+        pl.when(i < steps - DEPTH)(lambda: loads(i + DEPTH, lambda c: c.start()))
 
     for last in range(STORES):
-        stores(steps - STORES + last, lambda d: d.wait())
-
-
-def finish(news, grads, m, v):
+        stores(steps - STORES + last, lambda c: c.wait())
+
+
+def finish(news, grads, m, v, kept):
     shape = (2, CHIPS, 3, CHIPS)
     news, grads = news.reshape(*shape, 2, CHIPS, MR, LANE), grads.reshape(*shape, MR, LANE)
-    anywhere = pl.BlockSpec(memory_space=pl.ANY)
+    anywhere, here = pl.BlockSpec(memory_space=pltpu.HBM), pl.BlockSpec(memory_space=pltpu.VMEM)
     blocks = [(ROWS, PIECE), (ROWS, PIECE), (2 * SUB, D)]
     states = [jax.ShapeDtypeStruct(a.shape, F32) for a in m]
     return pl.pallas_call(
         finish_kernel,
         name="finish",
         out_shape=[*[jax.ShapeDtypeStruct((2, D, FF), BF)] * 2, jax.ShapeDtypeStruct((2, FF, D), BF), *states * 2],
-        in_specs=[anywhere] * 8,
+        in_specs=[anywhere] * 8 + [here] * len(kept),
         out_specs=[anywhere] * 9,
         scratch_shapes=[
             *[pltpu.VMEM((DEPTH, CHIPS, CHIPS, MR, LANE), BF)] * 3,
-            *[pltpu.VMEM((DEPTH, *b, LANE), BF) for b in ((CHIPS, ROWS), (CHIPS, ROWS), (2, MR))],
-            *[pltpu.VMEM((DEPTH, *b), F32) for b in blocks * 2],
+            *[pltpu.VMEM((DEPTH, n, MR, LANE), BF) for n in (CHIPS, CHIPS, 2)],
+            *[pltpu.VMEM((DEPTH, *blocks[0]), F32)] * 4,
             *[pltpu.VMEM((STORES, *b), BF) for b in ((ROWS, FF), (ROWS, FF), (TALL, D))],
             *[pltpu.VMEM((STORES, *b), F32) for b in blocks * 2],
             pltpu.SemaphoreType.DMA((DEPTH, 3, 4)), pltpu.SemaphoreType.DMA((STORES, 3, 3)),
         ],
-        compiler_params=pltpu.CompilerParams(vmem_limit_bytes=60 * 2**20),
-    )(news, grads, *m, *v)
+        compiler_params=pltpu.CompilerParams(vmem_limit_bytes=18 * 2**20),
+    )(*in_hbm((news, grads, *m, *v)), *[pltpu.with_memory_space_constraint(a, pltpu.VMEM) for a in kept])
 
 
 def solution(mesh):
     def step(x, dy, *arrays):
         weights, m, v = (arrays[i : i + 3] for i in (0, 3, 6))
-        news, grads, *_ = backward(x[0], dy[0], weights, m, v)
-        return tuple(finish(news, grads, m, v))
+        news, grads, _, *kept = backward(x[0], dy[0], weights, m, v)
+        return tuple(finish(news, grads, m, v, kept))
 
     by_device, whole, rows = P(("rep", "dp")), P(), P(None, "dp")
     return jax.shard_map(

time: 462 us -> 455 us (0.985)
  Pallas kernels: 461 us -> 454 us
    pallas_call x1, Pallas kernels: 34 us -> 27.2 us  [finish(): pl.pallas_call(finish_kernel, name='finish', out_shape=[*[jax.ShapeDtypeS...]
where the time goes in v5:
time: 455 us
  Pallas kernels  454 us (100%)
    pallas_call x1, Pallas kernels, backward(): pl.pallas_call(kernel, name='backward', out_shape=[*[jax.ShapeDtypeStruct...  427 us
    pallas_call x1, Pallas kernels, finish(): pl.pallas_call(finish_kernel, name='finish', out_shape=[*[jax.ShapeDtypeS...  27.2 us

profile of v5, /device:TPU:0, one launch (start us, length us, event | category | flops | bytes accessed | tf_op | source)
XLA Modules:
  0.0 454.8 jit_solution(8841944533567859123)
XLA Ops:
  0.6 426.7 %backward.1 = (bf16[96,2,4,160,128]{4,3,2,1,0:T(8,128)(2,1)}, bf16[96,160,128]{2,1,0:T(8,128)(2,1)}, bf16[96,2,4,160,128]{4,3,2,1,0:T(8,128)(2,1)}, bf16[2048,10...) custom-call(bf16[2048,640]{1,0:T(8,128)(2,1)} %bitcast.6, ...), custom_call_target="tpu_custom_call" | custom-call | tf_op jit(solution)/shard_map/backward/pallas_call | solution.py:568
  427.4 27.2 %finish.1 = (bf16[2,640,4096]{2,1,0:T(8,128)(2,1)}, bf16[2,640,4096]{2,1,0:T(8,128)(2,1)}, bf16[2,4096,640]{2,1,0:T(8,128)(2,1)}, f32[2,80,4096]{2,1,0:T(8,128)}...) custom-call(bf16[2,4,3,4,2,4,160,128]{7,6,5,4,3,2,1,0:T(8,128)(2,1)}, ...), custom_call_target="tpu_custom_call" | custom-call | tf_op jit(solution)/shard_map/finish/pallas_call | solution.py:715

commit v6 on v5

--- a/solution.py
+++ b/solution.py
@@ -18,7 +18,7 @@
 
 ROUNDS, MR, SUB = 96, 160, 32
 PER_TILE = 12
-D0, LAG, LAGF, LAGA, LAGD = 1, 2, 2, 2, 2
+D0, LAG, LAGF, LAGA, LAGD = 1, 2, 3, 3, 2
 RING, SLOTS, KEPT = 16, 4, 12
 TICKS = ROUNDS + D0 + 3 * LAG + LAGF + 2 * LAGA + max(LAGD, SLOTS)
 AHEAD = 6

time: 455 us -> 452 us (level)
  no operation moved by 1% of the time
where the time goes in v6:
time: 452 us
  Pallas kernels  451 us (100%)
    pallas_call x1, Pallas kernels, backward(): pl.pallas_call(kernel, name='backward', out_shape=[*[jax.ShapeDtypeStruct...  424 us
    pallas_call x1, Pallas kernels, finish(): pl.pallas_call(finish_kernel, name='finish', out_shape=[*[jax.ShapeDtypeS...  27.2 us

profile of v6, /device:TPU:0, one launch (start us, length us, event | category | flops | bytes accessed | tf_op | source)
XLA Modules:
  0.0 452.2 jit_solution(521218469644784248)
XLA Ops:
  0.6 424.2 %backward.1 = (bf16[96,2,4,160,128]{4,3,2,1,0:T(8,128)(2,1)}, bf16[96,160,128]{2,1,0:T(8,128)(2,1)}, bf16[96,2,4,160,128]{4,3,2,1,0:T(8,128)(2,1)}, bf16[2048,10...) custom-call(bf16[2048,640]{1,0:T(8,128)(2,1)} %bitcast.6, ...), custom_call_target="tpu_custom_call" | custom-call | tf_op jit(solution)/shard_map/backward/pallas_call | solution.py:568
  424.8 27.2 %finish.1 = (bf16[2,640,4096]{2,1,0:T(8,128)(2,1)}, bf16[2,640,4096]{2,1,0:T(8,128)(2,1)}, bf16[2,4096,640]{2,1,0:T(8,128)(2,1)}, f32[2,80,4096]{2,1,0:T(8,128)}...) custom-call(bf16[2,4,3,4,2,4,160,128]{7,6,5,4,3,2,1,0:T(8,128)(2,1)}, ...), custom_call_target="tpu_custom_call" | custom-call | tf_op jit(solution)/shard_map/finish/pallas_call | solution.py:715
